TPU v7x, 32 devices: a whole 2x2x4 slice. The times are simulated.
32 devices in a mesh: row: 8 (over z, x), col: 4 (over y, core).
Axes of the slice: x: 2, y: 2, z: 4, core: 2. Of those that a mesh axis runs over, the one named last changes fastest.
Arguments:
- normal_matrix: float32 [4096, 4096], P('row', 'col'), as said below
Outputs:
- factored: float32 [4096, 4096], P('row', 'col')
- log_det: float32 [], replicated
Inputs may be any that keep to these rules, and one draw needn't show every extreme that they name: normal_matrix is symmetric and positive definite.
All inputs are finite; a program needn't handle non-finite values.
Results may differ from a plain program's by a relative error of at most 0.0001.
Values sent between devices are 32-bit elements; how exact they have to be, the bound alone decides.
A program may use at most 64 MiB of HBM per device.

v0:
```python
import functools

import jax
import jax.numpy as jnp
from jax import lax
from jax.experimental import pallas as pl
from jax.experimental.pallas import tpu as pltpu
from jax.sharding import PartitionSpec as P

MESH = pl.DeviceIdType.MESH
NB = 128
CHUNKS = 16
VMEM = pl.BlockSpec(memory_space=pltpu.VMEM)


def dot_nt(a, b):
    return lax.dot_general(
        a, b, (((1,), (1,)), ((), ())), precision=lax.Precision.HIGHEST,
        preferred_element_type=jnp.float32,
    )


def dot_nn(a, b):
    return lax.dot_general(
        a, b, (((1,), (0,)), ((), ())), precision=lax.Precision.HIGHEST,
        preferred_element_type=jnp.float32,
    )


def split(a):
    high = a.astype(jnp.bfloat16)
    return high, (a - high.astype(jnp.float32)).astype(jnp.bfloat16)


def dot_nt_split(a, b):
    def dot(u, v):
        return lax.dot_general(u, v, (((1,), (1,)), ((), ())), preferred_element_type=jnp.float32)

    return dot(a[0], b[0]) + (dot(a[0], b[1]) + dot(a[1], b[0]))


def solve(rows, w_ref):
    size = w_ref.shape[0]
    half = size // 2
    return jnp.concatenate(
        [dot_nt(rows[:, : e], w_ref[e - half : e, :e]) for e in range(half, size + 1, half)], axis=1
    )


def factor_block(a, hook):
    groups = NB // 8
    lane = lax.broadcasted_iota(jnp.int32, (8, NB), 1)
    sub = lax.broadcasted_iota(jnp.int32, (8, NB), 0)
    left = [a[8 * g : 8 * g + 8, :] for g in range(groups)]
    right = [(lane == sub + 8 * g).astype(jnp.float32) for g in range(groups)]
    upper, inverse, pivots = [], [], []

    def row(x, t):
        return jnp.broadcast_to(x[t : t + 1, :], (8, NB))

    def column(x, t):
        return jnp.broadcast_to(x[:, t : t + 1], (8, NB))

    for p in range(groups):
        if p and p % (groups // 4) == 0:
            hook(p // (groups // 4) - 1)
        first = 8 * p
        v, i = left[p], right[p]
        cols = [column(v, first + t) for t in range(8)]
        mult = {g: [column(left[g], first + t) for t in range(8)] for g in range(p + 1, groups)}
        u_rows, i_rows, d_rows = v, i, cols[0]
        for t in range(8):
            here = sub == t
            pivot = row(cols[t], t)
            if t:
                u_rows = jnp.where(here, v, u_rows)
                i_rows = jnp.where(here, i, i_rows)
            d_rows = jnp.where(here, pivot, d_rows)
            recip = 1.0 / pivot
            factor = jnp.where(here, -recip, cols[t] * recip)
            for u in range(t + 1, 8):
                cols[u] = jnp.where(here, 0.0, cols[u]) - factor * row(cols[u], t)
            v = jnp.where(here, 0.0, v) - factor * row(v, t)
            i = jnp.where(here, 0.0, i) - factor * row(i, t)
        scale = lax.rsqrt(d_rows)
        upper.append(jnp.where(lane >= sub + first, u_rows * scale, 0.0))
        inverse.append(i_rows * scale)
        pivots.append(d_rows)
        v_rows = [row(v, t) for t in range(8)]
        i_rows = [row(i, t) for t in range(8)]
        for g in range(p + 1, groups):
            left_sum = mult[g][0] * v_rows[0]
            right_sum = mult[g][0] * i_rows[0]
            for t in range(1, 8):
                left_sum = left_sum + mult[g][t] * v_rows[t]
                right_sum = right_sum + mult[g][t] * i_rows[t]
            left[g] = left[g] - left_sum
            right[g] = right[g] - right_sum
    return jnp.concatenate(upper, 0), jnp.concatenate(inverse, 0), jnp.concatenate(pivots, 0)


def factor_all(a_ref, l_ref, w_ref, logdet_ref, work, upper, inverse, pivot, relay):
    size = a_ref.shape[0]
    for end in range(NB, size + 1, NB):
        work[end - NB : end, :end] = a_ref[end - NB : end, :end]
    l_ref[...] = jnp.zeros_like(l_ref)
    w_ref[...] = jnp.zeros_like(w_ref)

    @pl.loop(0, size // NB)
    def _(step):
        span = pl.ds(pl.multiple_of(step * NB, NB), NB)
        r, w, d = factor_block(work[span, span], lambda n: relay(4 * step + n))
        upper[...] = r
        inverse[...] = w
        pivot[span, :] = d
        w_ref[span, span] = inverse[...]
        l_ref[span, span] = upper[...].T
        relay(4 * step + 3)
        for p in range(size // NB):

            @pl.when(step == p)
            def _():
                at = slice(p * NB, (p + 1) * NB)
                end = (p + 1) * NB
                if p:
                    inner = dot_nn(l_ref[at, : p * NB], w_ref[: p * NB, : p * NB])
                    w_ref[at, : p * NB] = -dot_nn(inverse[...], inner)
                if end < size:
                    panel = dot_nt(work[end:, at], inverse[...])
                    l_ref[end:, at] = panel
                    for col in range(end, size, NB):
                        block = panel[col - end : col - end + NB, :]
                        work[col:, col : col + NB] = work[col:, col : col + NB] - dot_nt(panel[col - end :, :], block)

    logdet_ref[...] = jnp.sum(jnp.log(pivot[...]), axis=0, keepdims=True)


def update_kernel(mine_ref, panel_ref, other_ref, l_ref, out_ref):
    r, c = lax.axis_index("row"), lax.axis_index("col")
    leading = (c == 0) & (pl.program_id(0) == 0)

    @pl.when(r == 0)
    def _():
        out_ref[...] = jnp.where(leading, l_ref[...], 0.0)

    @pl.when((r > 0) & leading)
    def _():
        out_ref[...] = panel_ref[...]

    @pl.when((r > 0) & jnp.logical_not(leading))
    def _():
        update = dot_nt_split(split(panel_ref[...]), split(other_ref[...]))
        out_ref[...] = mine_ref[...] - update


def panel_kernel(mine_ref, panel_ref, other_ref, l_ref, logdet_ref, own_ref, cols_ref, w_ref, diag_ref, work, upper, inverse, pivot,
                 load_sem, own_send, own_recv, diag_send, diag_recv, cols_send, cols_recv, keep_sem):
    rows, columns = lax.axis_size("row"), lax.axis_size("col")
    r, c = lax.axis_index("row"), lax.axis_index("col")
    q, x = r // 2, r % 2
    other = r + 1 - 2 * x
    width = own_ref.shape[0]
    piece = width // CHUNKS
    even = c % 2 == 0

    links = [
        ((r, c - 1), c >= 1), ((r, c + 1), c + 1 < columns),
        ((r, c - 2), c >= 2), ((r, c + 2), c + 2 < columns),
        ((r - 2, c), r >= 2), ((r + 2, c), r + 2 < rows),
        ((other, c), other >= 0),
    ]
    barrier = pltpu.get_barrier_semaphore()
    for device, exists in links:
        @pl.when(exists)
        def _():
            pl.semaphore_signal(barrier, inc=1, device_id=device, device_id_type=MESH)
    peers = sum(jnp.where(exists, 1, 0).astype(jnp.int32) for _, exists in links)
    pl.semaphore_wait(barrier, peers)

    def part(ref, i, base=0):
        return ref.at[pl.ds(pl.multiple_of(base + i * piece, piece), piece), :]

    def low(ref, i):
        seen = -(-((i + 1) * piece) // NB) * NB
        return ref.at[pl.ds(i * piece, piece), pl.ds(0, seen)]

    def send(source, target, send_sem, recv_sem, device):
        return pltpu.make_async_remote_copy(
            src_ref=source, dst_ref=target, send_sem=send_sem, recv_sem=recv_sem,
            device_id=device, device_id_type=MESH,
        )

    def load(i):
        return pltpu.make_async_copy(
            mine_ref.at[pl.ds(i * piece, piece), pl.ds(0, width)], part(own_ref, i), load_sem.at[i]
        )

    base_x = pl.multiple_of(x * width, width)
    base_o = pl.multiple_of((1 - x) * width, width)
    sends = []

    def forward(condition, *args):
        copy = send(*args)
        sends.append((condition, copy))

        @pl.when(condition)
        def _():
            copy.start()

    def spread(i, source):
        target = part(cols_ref, i, base_x)
        return [
            ((q >= c) & (r + 2 < rows), send(source, target, cols_send.at[0, i], cols_recv.at[0, i], (r + 2, c))),
            ((q <= c) & (q > 0), send(source, target, cols_send.at[1, i], cols_recv.at[0, i], (r - 2, c))),
            (q >= 0, send(source, target, cols_send.at[2, i], cols_recv.at[1, i], (other, c))),
        ]

    def start(condition, copies):
        for exists, copy in copies:
            @pl.when(condition & exists)
            def _():
                copy.start()

    def relay(i):
        target = part(cols_ref, i, base_x)

        @pl.when(q != c)
        def _():
            send(target, target, cols_send.at[0, i], cols_recv.at[0, i], (other, c)).wait_recv()

        start(q != c, spread(i, target))

    def own_part(i):
        return send(part(own_ref, i), part(own_ref, i), own_send.at[0, i], own_recv.at[i], (r, c + 1))

    @pl.when(c == 0)
    def _():
        for i in range(CHUNKS):
            load(i).start()

    for i in range(CHUNKS):
        @pl.when(c == 0)
        def _():
            load(i).wait()

        @pl.when(c > 0)
        def _():
            own_part(i).wait_recv()

        piece_ref = part(own_ref, i)
        forward(even & (c + 2 < columns), piece_ref, piece_ref, own_send.at[0, i], own_recv.at[i], (r, c + 2))
        forward(even, piece_ref, piece_ref, own_send.at[1, i], own_recv.at[i], (r, c + 1))
        low_ref = low(own_ref, i)
        forward((r == 0) & even & (rows > 2), low_ref, low(diag_ref, i), diag_send.at[0, i], diag_recv.at[i], (r + 2, c))
        forward((r == 0) & even, low_ref, low(diag_ref, i), diag_send.at[1, i], diag_recv.at[i], (r + 1, c))
        keep = pltpu.make_async_copy(low_ref, low(diag_ref, i), keep_sem.at[0, i])

        @pl.when(r == 0)
        def _():
            keep.start()

        start(q == c, spread(i, piece_ref))
        keep_cols = pltpu.make_async_copy(piece_ref, part(cols_ref, i, base_x), keep_sem.at[1, i])

        @pl.when(q == c)
        def _():
            keep_cols.start()

    for i in range(CHUNKS):
        diag_piece = low(diag_ref, i)
        incoming = send(diag_piece, diag_piece, diag_send.at[0, i], diag_recv.at[i], (other, c))

        @pl.when(r > 0)
        def _():
            incoming.wait_recv()

        forward((r > 0) & even & (x == 0) & (r + 2 < rows), diag_piece, diag_piece, diag_send.at[0, i], diag_recv.at[i], (r + 2, c))
        forward((r > 0) & even & (x == 0), diag_piece, diag_piece, diag_send.at[1, i], diag_recv.at[i], (r + 1, c))
        forward((r > 0) & even, diag_piece, diag_piece, diag_send.at[2, i], diag_recv.at[i], (r, c + 1))

    for i in range(CHUNKS):
        @pl.when(r == 0)
        def _():
            pltpu.make_async_copy(low(own_ref, i), low(diag_ref, i), keep_sem.at[0, i]).wait()

    factor_all(diag_ref, l_ref, w_ref, logdet_ref, work, upper, inverse, pivot, relay)

    span_x, span_o = pl.ds(base_x, width), pl.ds(base_o, width)
    panel_ref[...] = solve(own_ref[...], w_ref)
    for i in range(CHUNKS):
        @pl.when(q == c)
        def _():
            pltpu.make_async_copy(part(own_ref, i), part(cols_ref, i, base_x), keep_sem.at[1, i]).wait()

    other_ref[span_x, :] = solve(cols_ref[span_x, :], w_ref)
    for i in range(CHUNKS):
        target = part(cols_ref, i, base_o)
        send(target, target, cols_send.at[2, i], cols_recv.at[1, i], (other, c)).wait_recv()
    other_ref[span_o, :] = solve(cols_ref[span_o, :], w_ref)
    for i in range(CHUNKS):
        sends += spread(i, part(cols_ref, i, base_x))
    for condition, copy in sends:
        @pl.when(condition)
        def _():
            copy.wait_send()


def panel_step(mine):
    width = mine.shape[0]
    square = jax.ShapeDtypeStruct((width, width), jnp.float32)
    dma = pltpu.SemaphoreType.DMA
    return pl.pallas_call(
        panel_kernel,
        out_shape=(
            square, jax.ShapeDtypeStruct((2 * width, width), jnp.float32), square,
            jax.ShapeDtypeStruct((1, NB), jnp.float32),
        ),
        in_specs=[pl.BlockSpec(memory_space=pl.ANY)],
        out_specs=(VMEM,) * 4,
        scratch_shapes=[
            pltpu.VMEM((width, width), jnp.float32), pltpu.VMEM((2 * width, width), jnp.float32),
            pltpu.VMEM((width, width), jnp.float32), pltpu.VMEM((width, width), jnp.float32),
            pltpu.VMEM((width, width), jnp.float32),
            pltpu.VMEM((NB, NB), jnp.float32), pltpu.VMEM((NB, NB), jnp.float32),
            pltpu.VMEM((width, NB), jnp.float32),
            dma((CHUNKS,)), dma((2, CHUNKS)), dma((CHUNKS,)), dma((3, CHUNKS)), dma((CHUNKS,)),
            dma((3, CHUNKS)), dma((2, CHUNKS)), dma((2, CHUNKS)),
        ],
        compiler_params=pltpu.CompilerParams(collective_id=0, has_side_effects=True),
    )(mine)


def per_device(mine):
    panel, other, l, logdet = panel_step(mine)
    width = mine.shape[0]
    across = pl.BlockSpec((width, width), lambda s: (0, s))
    whole = pl.BlockSpec((width, width), lambda s: (0, 0))
    block = pl.pallas_call(
        update_kernel,
        grid=(mine.shape[1] // width,),
        out_shape=jax.ShapeDtypeStruct(mine.shape, jnp.float32),
        in_specs=[across, whole, pl.BlockSpec((width, width), lambda s: (s, 0)), whole],
        out_specs=across,
    )(mine, panel, other, l)
    return block, logdet[0, 0]


def solution(mesh):
    return jax.shard_map(
        per_device, mesh=mesh, in_specs=(P("row", "col"),), out_specs=(P("row", "col"), P()), check_vma=False
    )
```

profile of v0, /device:TPU:7, one launch (start us, length us, event | category | flops | bytes accessed | tf_op | source)
XLA Modules:
  0.0 78.3 jit_solution(14290322482614356245)
XLA Ops:
  0.6 71.2 %shard_map.30 = (f32[512,512]{1,0:T(8,128)}, f32[1024,512]{1,0:T(8,128)}, f32[512,512]{1,0:T(8,128)}, f32[1,128]{1,0:T(1,128)}) custom-call(f32[512,1024]{1,0:T(8,128)} %mine_ref.3), custom_call_target="tpu_custom_call" | custom-call | tf_op jit(solution)/shard_map/pallas_call | solution.py:312
  71.8 0.0 copy-start
  71.8 5.3 %shard_map.31 = f32[512,1024]{1,0:T(8,128)} custom-call(f32[512,1024]{1,0:T(8,128)} %mine_ref.3, f32[512,512]{1,0:T(8,128)} %get-tuple-element.6.panel_ref, f32[1024,512]{1,0:T(8,128)} %get-tuple-element.7.other_ref, f32[512,512]{1,0:T(8,128)} %get-tuple-element.8.l_ref), custom_call_target="tpu_custom_call" | custom-call | tf_op jit(solution)/shard_map/pallas_call | solution.py:338
  77.1 0.0 copy-done
Async XLA Ops:
  71.8 5.3 %copy-start = (f32[1,128]{1,0:T(1,128)S(1)}, f32[1,128]{1,0:T(1,128)}, u32[]{:S(2)}) copy-start(f32[1,128]{1,0:T(1,128)} %get-tuple-element.9) | copy-start | bytes 1540
where the time goes:
time: 78.4 us; the launch traced here: 78.3 us
  Pallas kernels  76.4 us (97%)
  between operations  1.81 us (2%)
    pallas_call x1, Pallas kernels, panel_step(): pl.pallas_call(panel_kernel, out_shape=(square, jax.ShapeDtypeStruct((2 *...  71.2 us
    pallas_call x1, Pallas kernels, per_device(): pl.pallas_call(update_kernel, grid=(mine.shape[1] // width,), out_shape=j...  5.26 us

commit v1 on v0

v1 whole, which is shorter than its diff:
```python
import functools

import jax
import jax.numpy as jnp
from jax import lax
from jax.experimental import pallas as pl
from jax.experimental.pallas import tpu as pltpu
from jax.sharding import PartitionSpec as P

MESH = pl.DeviceIdType.MESH
NB = 128
CHUNKS = 32
SLOTS = 8
LEAD = 6
LAG = 10
STARTS = 4
PANELS = 8
VMEM = pl.BlockSpec(memory_space=pltpu.VMEM)


def dot_nt(a, b):
    return lax.dot_general(
        a, b, (((1,), (1,)), ((), ())), precision=lax.Precision.HIGHEST,
        preferred_element_type=jnp.float32,
    )


def dot_nn(a, b):
    return lax.dot_general(
        a, b, (((1,), (0,)), ((), ())), precision=lax.Precision.HIGHEST,
        preferred_element_type=jnp.float32,
    )


def split(a):
    high = a.astype(jnp.bfloat16)
    return high, (a - high.astype(jnp.float32)).astype(jnp.bfloat16)


def dot_split(a, b, axis):
    def dot(u, v):
        return lax.dot_general(u, v, (((1,), (axis,)), ((), ())), preferred_element_type=jnp.float32)

    return dot(a[0], b[0]) + (dot(a[0], b[1]) + dot(a[1], b[0]))


def factor_block(a, hook):
    groups = NB // 8
    lane = lax.broadcasted_iota(jnp.int32, (8, NB), 1)
    sub = lax.broadcasted_iota(jnp.int32, (8, NB), 0)
    left = [a[8 * g : 8 * g + 8, :] for g in range(groups)]
    right = [(lane == sub + 8 * g).astype(jnp.float32) for g in range(groups)]
    upper, inverse, pivots = [], [], []

    def row(x, t):
        return jnp.broadcast_to(x[t : t + 1, :], (8, NB))

    def column(x, t):
        return jnp.broadcast_to(x[:, t : t + 1], (8, NB))

    for p in range(groups):
        if p and p % (groups // SLOTS) == 0:
            hook(p // (groups // SLOTS) - 1)
        first = 8 * p
        v, i = left[p], right[p]
        cols = [column(v, first + t) for t in range(8)]
        mult = {g: [column(left[g], first + t) for t in range(8)] for g in range(p + 1, groups)}
        u_rows, i_rows, d_rows = v, i, cols[0]
        for t in range(8):
            here = sub == t
            pivot = row(cols[t], t)
            if t:
                u_rows = jnp.where(here, v, u_rows)
                i_rows = jnp.where(here, i, i_rows)
            d_rows = jnp.where(here, pivot, d_rows)
            recip = 1.0 / pivot
            factor = jnp.where(here, -recip, cols[t] * recip)
            for u in range(t + 1, 8):
                cols[u] = jnp.where(here, 0.0, cols[u]) - factor * row(cols[u], t)
            v = jnp.where(here, 0.0, v) - factor * row(v, t)
            i = jnp.where(here, 0.0, i) - factor * row(i, t)
        scale = lax.rsqrt(d_rows)
        upper.append(jnp.where(lane >= sub + first, u_rows * scale, 0.0))
        inverse.append(i_rows * scale)
        pivots.append(d_rows)
        v_rows = [row(v, t) for t in range(8)]
        i_rows = [row(i, t) for t in range(8)]
        for g in range(p + 1, groups):
            left_sum = mult[g][0] * v_rows[0]
            right_sum = mult[g][0] * i_rows[0]
            for t in range(1, 8):
                left_sum = left_sum + mult[g][t] * v_rows[t]
                right_sum = right_sum + mult[g][t] * i_rows[t]
            left[g] = left[g] - left_sum
            right[g] = right[g] - right_sum
    return jnp.concatenate(upper, 0), jnp.concatenate(inverse, 0), jnp.concatenate(pivots, 0)


def factor_all(a_ref, l_ref, w_ref, logdet_ref, work, upper, inverse, pivot, slot):
    size = a_ref.shape[0]
    work[:NB, :NB] = a_ref[:NB, :NB]
    l_ref[...] = jnp.zeros_like(l_ref)
    w_ref[...] = jnp.zeros_like(w_ref)

    @pl.loop(0, size // NB)
    def _(step):
        span = pl.ds(pl.multiple_of(step * NB, NB), NB)
        r, w, d = factor_block(work[span, span], lambda n: slot(step, n))
        upper[...] = r
        inverse[...] = w
        pivot[span, :] = d
        w_ref[span, span] = inverse[...]
        l_ref[span, span] = upper[...].T
        slot(step, SLOTS - 1)
        for p in range(size // NB):

            @pl.when(step == p)
            def _():
                at = slice(p * NB, (p + 1) * NB)
                end = (p + 1) * NB
                if p:
                    inner = dot_nn(l_ref[at, : p * NB], w_ref[: p * NB, : p * NB])
                    w_ref[at, : p * NB] = -dot_nn(inverse[...], inner)
                if end < size:
                    below = work[end:, at] if p else a_ref[end:, at]
                    l_ref[end:, at] = dot_nt(below, inverse[...])
                    following = slice(end, end + NB)
                    work[end:, following] = a_ref[end:, following] - dot_nt(l_ref[end:, :end], l_ref[following, :end])

    logdet_ref[...] = jnp.sum(jnp.log(pivot[...]), axis=0, keepdims=True)


def update_kernel(mine_ref, panel_ref, other_ref, l_ref, out_ref):
    r, c = lax.axis_index("row"), lax.axis_index("col")
    leading = (c == 0) & (pl.program_id(0) == 0)

    @pl.when(r == 0)
    def _():
        out_ref[...] = jnp.where(leading, l_ref[...], 0.0)

    @pl.when((r > 0) & leading)
    def _():
        out_ref[...] = panel_ref[...]

    @pl.when((r > 0) & jnp.logical_not(leading))
    def _():
        out_ref[...] = mine_ref[...] - dot_split(split(panel_ref[...]), split(other_ref[...]), 0)


def panel_kernel(mine_ref, panel_ref, other_ref, l_ref, logdet_ref, own_ref, cols_ref, w_ref, diag_ref, work, upper, inverse, pivot,
                 diag_send, diag_recv, own_send, own_recv, cols_send, cols_recv):
    rows, columns = lax.axis_size("row"), lax.axis_size("col")
    r, c = lax.axis_index("row"), lax.axis_index("col")
    q, x = r // 2, r % 2
    other = r + 1 - 2 * x
    partner = c + 1 - 2 * (c % 2)
    odd = c % 2 == 1
    width = own_ref.shape[0]
    top = r == 0
    corner = top & (c == 0)

    links = [
        ((r, partner), partner >= 0), ((other, c), other >= 0),
        ((r - 2, c), r >= 2), ((r + 2, c), r + 2 < rows),
        ((r, c - 2), c >= 2), ((r, c + 2), c + 2 < columns),
    ]
    barrier = pltpu.get_barrier_semaphore()
    for device, exists in links:
        @pl.when(exists)
        def _():
            pl.semaphore_signal(barrier, inc=1, device_id=device, device_id_type=MESH)
    peers = sum(jnp.where(exists, 1, 0).astype(jnp.int32) for _, exists in links)
    pl.semaphore_wait(barrier, peers)

    def send(source, target, send_sem, recv_sem, device):
        return pltpu.make_async_remote_copy(
            src_ref=source, dst_ref=target, send_sem=send_sem, recv_sem=recv_sem,
            device_id=device, device_id_type=MESH,
        )

    def start(condition, copies):
        for exists, copy in copies:
            @pl.when(condition & exists)
            def _():
                copy.start()

    def drain(condition, copies):
        for exists, copy in copies:
            @pl.when(condition & exists)
            def _():
                copy.wait_send()

    tall = NB // STARTS
    tiles = [(pl.ds(i * tall, tall), pl.ds(0, NB)) for i in range(STARTS)]
    tiles += [
        (pl.ds(i * NB, NB), pl.ds(j * NB, NB)) for j in range(width // NB) for i in range(j, width // NB) if i
    ]
    side_row = jnp.where(x == 0, r + 1, r - 2)
    has_side = ((x == 0) & (q >= 1)) | (r == 3)

    def diag_load(k):
        return pltpu.make_async_copy(mine_ref.at[tiles[k]], diag_ref.at[tiles[k]], diag_recv.at[k])

    def diag_copies(k):
        tile = diag_ref.at[tiles[k]]

        def to(n, device):
            return send(tile, tile, diag_send.at[n, k], diag_recv.at[k], device)

        return [
            ((c == 1) & (x == 0) & (r + 2 < rows), to(0, (r + 2, c))),
            ((c == 1) & has_side, to(1, (side_row, c))),
            (odd & (c + 2 < columns), to(2, (r, c + 2))),
            (odd & jnp.logical_not(top & (c == 1)), to(3, (r, c - 1))),
        ]

    def diag_first(k):
        return send(mine_ref.at[tiles[k]], diag_ref.at[tiles[k]], diag_send.at[0, k], diag_recv.at[k], (r, c + 1))

    def diag_step(k):
        @pl.when(corner)
        def _():
            diag_load(k).wait()

        @pl.when(jnp.logical_not(corner))
        def _():
            diag_copies(k)[0][1].wait_recv()

        start(odd, diag_copies(k))

    deep = width // PANELS
    everyone = pl.ds(0, width)

    def own_part(j):
        return own_ref.at[pl.ds(pl.multiple_of(j * deep, deep), deep), :]

    def own_copies(j, source):
        return [
            (c + 2 < columns, send(source, own_part(j), own_send.at[0, j], own_recv.at[j], (r, c + 2))),
            (c >= 0, send(source, own_part(j), own_send.at[1, j], own_recv.at[j], (r, c + 1))),
        ]

    def own_source(j):
        return mine_ref.at[pl.ds(pl.multiple_of(j * deep, deep), deep), everyone]

    def own_load(j):
        return pltpu.make_async_copy(own_source(j), own_part(j), own_recv.at[j])

    def own_relay(j):
        own_copies(j, own_part(j))[0][1].wait_recv()
        start(c >= 0, own_copies(j, own_part(j)))

    below = jnp.logical_not(top)
    own_relays = below & (c > 0) & jnp.logical_not(odd)

    piece = width // CHUNKS

    def cols_part(ref, half, i):
        return ref.at[pl.ds(pl.multiple_of(i * piece, piece), piece), pl.ds(half * width, width)]

    def cols_copies(half, i, source):
        def to(n, device):
            return send(source, cols_part(cols_ref, half, i), cols_send.at[2 * half + n, i], cols_recv.at[half, i], device)

        if half == 0:
            return [((x == 0) & (r + 2 < rows), to(0, (r + 2, c))), (has_side, to(1, (side_row, c)))]
        return [((x == 1) & (r + 2 < rows), to(0, (r + 2, c))), ((x == 1) & (q >= 1), to(1, (r - 1, c)))]

    def cols_first(half, i):
        source = cols_part(mine_ref, half, i)
        if half == 0:
            return cols_copies(0, i, source)[0][1]
        return send(source, cols_part(cols_ref, 1, i), cols_send.at[2, i], cols_recv.at[1, i], (r + 1, c))

    def cols_start(condition):
        @pl.when(condition)
        def _():
            @pl.loop(0, CHUNKS)
            def _(i):
                cols_first(1, i).start()

                @pl.when(c > 0)
                def _():
                    cols_first(0, i).start()

    def cols_wait(half, i):
        cols_copies(half, i, cols_part(cols_ref, half, i))[0][1].wait_recv()

    def cols_relay(half, i, condition):
        @pl.when(condition)
        def _():
            cols_wait(half, i)
            start(c >= 0, cols_copies(half, i, cols_part(cols_ref, half, i)))

    relays = [below & (c > 0) & (((x == 0) & (q >= 1)) | (r == 3)), x == 1]
    lead = jnp.where(r == 1, LEAD, 0)

    @pl.when(corner)
    def _():
        for k in range(len(tiles)):
            diag_first(k).start()
        for k in range(len(tiles)):
            diag_load(k).start()

    cols_start(top & (c != 1))

    @pl.when(below & (c == 0))
    def _():
        for j in range(PANELS):
            start(c >= 0, own_copies(j, own_source(j)))
        for j in range(PANELS):
            own_load(j).start()

    @pl.when(r == 1)
    def _():
        @pl.loop(0, LEAD)
        def _(i):
            cols_relay(1, i, x == 1)

    for k in range(STARTS):
        diag_step(k)

    early = top & (c <= 1)

    @pl.when(early)
    def _():
        for k in range(STARTS, len(tiles)):
            diag_step(k)

    cols_start(top & (c == 1))

    when = {(0, 0): 0, (0, 1): 1, (0, 2): 2, (0, 3): 3, (0, 4): 4, (0, 5): 5, (1, 0): 6, (1, 2): 7, (1, 4): 8}

    def slot(step, n):
        for (at_step, at_n), k in when.items():
            if at_n == n:
                @pl.when((step == at_step) & jnp.logical_not(early))
                def _():
                    diag_step(STARTS + k)
        at = SLOTS * step + n
        i = at + lead
        pair = 2 * (at - LAG)
        first = jnp.where(c == 1, pair, at)
        cols_relay(1, i, relays[1] & (i < CHUNKS))
        cols_relay(0, first, relays[0] & (first >= 0) & (first < CHUNKS))
        cols_relay(0, pair + 1, relays[0] & (c == 1) & (pair >= 0) & (pair < CHUNKS))
        if n % 2 == 1:
            j = (at - LAG - 1) // 2

            @pl.when(own_relays & (at > LAG) & (j < PANELS))
            def _():
                own_relay(j)

    factor_all(diag_ref, l_ref, w_ref, logdet_ref, work, upper, inverse, pivot, slot)

    @pl.when(below)
    def _():
        @pl.when(c == 0)
        def _():
            for j in range(PANELS):
                own_load(j).wait()

        @pl.when(odd)
        def _():
            for j in range(PANELS):
                own_copies(j, own_part(j))[0][1].wait_recv()

        half = width // 2
        own = split(own_ref[...])
        for e in range(half, width + 1, half):
            factor = split(w_ref[e - half : e, :e])
            panel_ref[:, e - half : e] = dot_split((own[0][:, :e], own[1][:, :e]), factor, 1)

        for n in range(2):
            @pl.when(jnp.logical_not(relays[n]) & ((c > 0) | (n == 1)))
            def _():
                @pl.loop(0, CHUNKS)
                def _(i):
                    cols_wait(n, i)

        cols = split(cols_ref[...])
        for e in range(half, width + 1, half):
            factor = split(w_ref[e - half : e, :e])
            other_ref[e - half : e, :] = dot_split(factor, (cols[0][:e, :], cols[1][:e, :]), 0)

    @pl.when(corner)
    def _():
        for k in range(len(tiles)):
            diag_first(k).wait_send()

    for k in range(len(tiles)):
        drain(odd, diag_copies(k))

    @pl.when(below & jnp.logical_not(odd))
    def _():
        @pl.loop(0, PANELS)
        def _(j):
            drain(c >= 0, own_copies(j, own_part(j)))

    @pl.loop(0, CHUNKS)
    def _(i):
        @pl.when(top)
        def _():
            cols_first(1, i).wait_send()

            @pl.when(c > 0)
            def _():
                cols_first(0, i).wait_send()

        for n in range(2):
            drain(relays[n], cols_copies(n, i, cols_part(cols_ref, n, i)))


def panel_step(mine):
    width = mine.shape[0]
    square = jax.ShapeDtypeStruct((width, width), jnp.float32)
    wide = (width, 2 * width)
    dma = pltpu.SemaphoreType.DMA
    tiles = (width // NB) * (width // NB + 1) // 2 - 1 + STARTS
    return pl.pallas_call(
        panel_kernel,
        out_shape=(
            square, jax.ShapeDtypeStruct(wide, jnp.float32), square,
            jax.ShapeDtypeStruct((1, NB), jnp.float32),
        ),
        in_specs=[pl.BlockSpec(memory_space=pl.ANY)],
        out_specs=(VMEM,) * 4,
        scratch_shapes=[
            pltpu.VMEM((width, width), jnp.float32), pltpu.VMEM(wide, jnp.float32),
            pltpu.VMEM((width, width), jnp.float32), pltpu.VMEM((width, width), jnp.float32),
            pltpu.VMEM((width, width), jnp.float32),
            pltpu.VMEM((NB, NB), jnp.float32), pltpu.VMEM((NB, NB), jnp.float32),
            pltpu.VMEM((width, NB), jnp.float32),
            dma((4, tiles)), dma((tiles,)), dma((2, PANELS)), dma((PANELS,)), dma((4, CHUNKS)), dma((2, CHUNKS)),
        ],
        compiler_params=pltpu.CompilerParams(collective_id=0, has_side_effects=True),
    )(mine)


def per_device(mine):
    panel, other, l, logdet = panel_step(mine)
    width = mine.shape[0]
    across = pl.BlockSpec((width, width), lambda s: (0, s))
    whole = pl.BlockSpec((width, width), lambda s: (0, 0))
    block = pl.pallas_call(
        update_kernel,
        grid=(mine.shape[1] // width,),
        out_shape=jax.ShapeDtypeStruct(mine.shape, jnp.float32),
        in_specs=[across, whole, across, whole],
        out_specs=across,
    )(mine, panel, other, l)
    return block, logdet[0, 0]


def solution(mesh):
    return jax.shard_map(
        per_device, mesh=mesh, in_specs=(P("row", "col"),), out_specs=(P("row", "col"), P()), check_vma=False
    )
```

time: 78.4 us -> 61.6 us (0.79)
  the two profiles are of different devices: /device:TPU:7 before, /device:TPU:28 now
where the time goes in v1:
time: 61.6 us; the launch traced here: 61.4 us
  Pallas kernels  59.6 us (97%)
  between operations  1.81 us (3%)
    pallas_call x1, Pallas kernels, panel_step(): pl.pallas_call(panel_kernel, out_shape=(square, jax.ShapeDtypeStruct(wide...  54.4 us
    pallas_call x1, Pallas kernels, per_device(): pl.pallas_call(update_kernel, grid=(mine.shape[1] // width,), out_shape=j...  5.2 us

profile of v1, /device:TPU:28, one launch (start us, length us, event | category | flops | bytes accessed | tf_op | source)
XLA Modules:
  0.0 61.4 jit_solution(14861312119080680001)
XLA Ops:
  0.6 54.4 %shard_map.30 = (f32[512,512]{1,0:T(8,128)}, f32[512,1024]{1,0:T(8,128)}, f32[512,512]{1,0:T(8,128)}, f32[1,128]{1,0:T(1,128)}) custom-call(f32[512,1024]{1,0:T(8,128)} %mine_ref.3), custom_call_target="tpu_custom_call" | custom-call | tf_op jit(solution)/shard_map/pallas_call | solution.py:420
  55.1 0.0 copy-start
  55.1 5.2 %shard_map.31 = f32[512,1024]{1,0:T(8,128)} custom-call(f32[512,1024]{1,0:T(8,128)} %mine_ref.3, f32[512,512]{1,0:T(8,128)} %get-tuple-element.6.panel_ref, f32[512,1024]{1,0:T(8,128)} %get-tuple-element.7.other_ref, f32[512,512]{1,0:T(8,128)} %get-tuple-element.8.l_ref), custom_call_target="tpu_custom_call" | custom-call | tf_op jit(solution)/shard_map/pallas_call | solution.py:445
  60.3 0.0 copy-done
Async XLA Ops:
  55.1 5.2 %copy-start = (f32[1,128]{1,0:T(1,128)S(1)}, f32[1,128]{1,0:T(1,128)}, u32[]{:S(2)}) copy-start(f32[1,128]{1,0:T(1,128)} %get-tuple-element.9) | copy-start | bytes 1540

commit v2 on v1

--- a/solution.py
+++ b/solution.py
@@ -9,27 +9,18 @@
 
 MESH = pl.DeviceIdType.MESH
 NB = 128
+BAND = 32
 CHUNKS = 32
 SLOTS = 8
-LEAD = 6
+LEAD = 8
+AHEAD = 3
 LAG = 10
 STARTS = 4
 PANELS = 8
+FIRST = 7
+HOP = 6
+LATEST = 15
 VMEM = pl.BlockSpec(memory_space=pltpu.VMEM)
-
-
-def dot_nt(a, b):
-    return lax.dot_general(
-        a, b, (((1,), (1,)), ((), ())), precision=lax.Precision.HIGHEST,
-        preferred_element_type=jnp.float32,
-    )
-
-
-def dot_nn(a, b):
-    return lax.dot_general(
-        a, b, (((1,), (0,)), ((), ())), precision=lax.Precision.HIGHEST,
-        preferred_element_type=jnp.float32,
-    )
 
 
 def split(a):
@@ -44,56 +35,94 @@
     return dot(a[0], b[0]) + (dot(a[0], b[1]) + dot(a[1], b[0]))
 
 
-def factor_block(a, hook):
-    groups = NB // 8
-    lane = lax.broadcasted_iota(jnp.int32, (8, NB), 1)
+def dot_nt(a, b):
+    return dot_split(split(a), split(b), 1)
+
+
+def dot_nn(a, b):
+    return dot_split(split(a), split(b), 0)
+
+
+def total(terms):
+    while len(terms) > 1:
+        terms = [a + b for a, b in zip(terms[::2], terms[1::2])]
+    return terms[0]
+
+
+def eliminate(left, right, base, hook):
     sub = lax.broadcasted_iota(jnp.int32, (8, NB), 0)
-    left = [a[8 * g : 8 * g + 8, :] for g in range(groups)]
-    right = [(lane == sub + 8 * g).astype(jnp.float32) for g in range(groups)]
+    left, right = list(left), list(right)
     upper, inverse, pivots = [], [], []
 
     def row(x, t):
-        return jnp.broadcast_to(x[t : t + 1, :], (8, NB))
+        return jnp.take_along_axis(x, jnp.full((8, NB), t, jnp.int32), axis=0)
 
     def column(x, t):
         return jnp.broadcast_to(x[:, t : t + 1], (8, NB))
 
-    for p in range(groups):
-        if p and p % (groups // SLOTS) == 0:
-            hook(p // (groups // SLOTS) - 1)
-        first = 8 * p
-        v, i = left[p], right[p]
-        cols = [column(v, first + t) for t in range(8)]
-        mult = {g: [column(left[g], first + t) for t in range(8)] for g in range(p + 1, groups)}
-        u_rows, i_rows, d_rows = v, i, cols[0]
-        for t in range(8):
-            here = sub == t
-            pivot = row(cols[t], t)
-            if t:
-                u_rows = jnp.where(here, v, u_rows)
-                i_rows = jnp.where(here, i, i_rows)
-            d_rows = jnp.where(here, pivot, d_rows)
+    for p in range(0, len(left), 2):
+        if p:
+            hook()
+        first = base + 8 * p
+        rest = range(p + 2, len(left))
+        cols = [[column(x, first + t) for x in left[p : p + 2]] for t in range(16)]
+        mult = {g: [column(left[g], first + t) for t in range(16)] for g in rest}
+        v, i = left[p : p + 2], right[p : p + 2]
+        u_rows, i_rows, d_rows = list(v), list(i), [None, None]
+        for t in range(16):
+            at, s = t // 8, t % 8
+            here = sub == s
+            pivot = row(cols[t][at], s)
+            if s:
+                u_rows[at] = jnp.where(here, v[at], u_rows[at])
+                i_rows[at] = jnp.where(here, i[at], i_rows[at])
+                d_rows[at] = jnp.where(here, pivot, d_rows[at])
+            else:
+                u_rows[at], i_rows[at], d_rows[at] = v[at], i[at], pivot
             recip = 1.0 / pivot
-            factor = jnp.where(here, -recip, cols[t] * recip)
-            for u in range(t + 1, 8):
-                cols[u] = jnp.where(here, 0.0, cols[u]) - factor * row(cols[u], t)
-            v = jnp.where(here, 0.0, v) - factor * row(v, t)
-            i = jnp.where(here, 0.0, i) - factor * row(i, t)
-        scale = lax.rsqrt(d_rows)
-        upper.append(jnp.where(lane >= sub + first, u_rows * scale, 0.0))
-        inverse.append(i_rows * scale)
-        pivots.append(d_rows)
-        v_rows = [row(v, t) for t in range(8)]
-        i_rows = [row(i, t) for t in range(8)]
-        for g in range(p + 1, groups):
-            left_sum = mult[g][0] * v_rows[0]
-            right_sum = mult[g][0] * i_rows[0]
-            for t in range(1, 8):
-                left_sum = left_sum + mult[g][t] * v_rows[t]
-                right_sum = right_sum + mult[g][t] * i_rows[t]
-            left[g] = left[g] - left_sum
-            right[g] = right[g] - right_sum
-    return jnp.concatenate(upper, 0), jnp.concatenate(inverse, 0), jnp.concatenate(pivots, 0)
+            factor = [x * recip for x in cols[t]]
+            factor[at] = jnp.where(here, -recip, factor[at])
+
+            def step(pair):
+                taken = row(pair[at], s)
+                kept = [jnp.where(here, 0.0, x) if h == at else x for h, x in enumerate(pair)]
+                return [x - f * taken for x, f in zip(kept, factor)]
+
+            for w in range(t + 1, 16):
+                cols[w] = step(cols[w])
+            v, i = step(v), step(i)
+        for h in range(2):
+            scale = lax.rsqrt(d_rows[h])
+            upper.append(u_rows[h] * scale)
+            inverse.append(i_rows[h] * scale)
+            pivots.append(d_rows[h])
+        v_rows = [row(v[t // 8], t % 8) for t in range(16)]
+        i_rows = [row(i[t // 8], t % 8) for t in range(16)]
+        for g in rest:
+            left[g] = left[g] - total([mult[g][t] * v_rows[t] for t in range(16)])
+            right[g] = right[g] - total([mult[g][t] * i_rows[t] for t in range(16)])
+    return upper, inverse, pivots
+
+
+def factor_block(a, hook):
+    lane = lax.broadcasted_iota(jnp.int32, (NB, NB), 1)
+    sub = lax.broadcasted_iota(jnp.int32, (NB, NB), 0)
+    left, right = a, (lane == sub).astype(jnp.float32)
+    upper, inverse, pivots = [], [], []
+    for base in range(0, NB, BAND):
+        if base:
+            hook()
+        rows = [slice(8 * g, 8 * g + 8) for g in range(BAND // 8)]
+        u, i, d = eliminate([left[x] for x in rows], [right[x] for x in rows], base, hook)
+        u, i = jnp.concatenate(u, 0), jnp.concatenate(i, 0)
+        upper.append(u)
+        inverse.append(i)
+        pivots += d
+        if base + BAND < NB:
+            change = dot_nn(u.T[base + BAND :, :], jnp.concatenate([u, i], 1))
+            left, right = left[BAND:] - change[:, :NB], right[BAND:] - change[:, NB:]
+    upper = jnp.where(lane >= sub, jnp.concatenate(upper, 0), 0.0)
+    return upper, jnp.concatenate(inverse, 0), jnp.concatenate(pivots, 0)
 
 
 def factor_all(a_ref, l_ref, w_ref, logdet_ref, work, upper, inverse, pivot, slot):
@@ -105,7 +134,8 @@
     @pl.loop(0, size // NB)
     def _(step):
         span = pl.ds(pl.multiple_of(step * NB, NB), NB)
-        r, w, d = factor_block(work[span, span], lambda n: slot(step, n))
+        numbers = iter(range(SLOTS - 1))
+        r, w, d = factor_block(work[span, span], lambda: slot(step, next(numbers)))
         upper[...] = r
         inverse[...] = w
         pivot[span, :] = d
@@ -130,7 +160,7 @@
     logdet_ref[...] = jnp.sum(jnp.log(pivot[...]), axis=0, keepdims=True)
 
 
-def update_kernel(mine_ref, panel_ref, other_ref, l_ref, out_ref):
+def update_kernel(rest_ref, panel_ref, other_ref, l_ref, out_ref):
     r, c = lax.axis_index("row"), lax.axis_index("col")
     leading = (c == 0) & (pl.program_id(0) == 0)
 
@@ -144,10 +174,11 @@
 
     @pl.when((r > 0) & jnp.logical_not(leading))
     def _():
-        out_ref[...] = mine_ref[...] - dot_split(split(panel_ref[...]), split(other_ref[...]), 0)
-
-
-def panel_kernel(mine_ref, panel_ref, other_ref, l_ref, logdet_ref, own_ref, cols_ref, w_ref, diag_ref, work, upper, inverse, pivot,
+        half = panel_ref.shape[1] // 2
+        out_ref[...] = rest_ref[...] - dot_nn(panel_ref[:, half:], other_ref[half:, :])
+
+
+def panel_kernel(mine_ref, panel_ref, other_ref, rest_ref, l_ref, logdet_ref, own_ref, cols_ref, w_ref, diag_ref, work, upper, inverse, pivot,
                  diag_send, diag_recv, own_send, own_recv, cols_send, cols_recv):
     rows, columns = lax.axis_size("row"), lax.axis_size("col")
     r, c = lax.axis_index("row"), lax.axis_index("col")
@@ -252,6 +283,7 @@
 
     below = jnp.logical_not(top)
     own_relays = below & (c > 0) & jnp.logical_not(odd)
+    own_lag = jnp.minimum(FIRST + HOP * (c // 2), LATEST)
 
     piece = width // CHUNKS
 
@@ -293,7 +325,8 @@
             start(c >= 0, cols_copies(half, i, cols_part(cols_ref, half, i)))
 
     relays = [below & (c > 0) & (((x == 0) & (q >= 1)) | (r == 3)), x == 1]
-    lead = jnp.where(r == 1, LEAD, 0)
+    lead = jnp.where(r == 1, LEAD, jnp.where(c > 1, AHEAD, 0))
+    lead_left = jnp.where(c > 1, AHEAD, 0)
 
     @pl.when(corner)
     def _():
@@ -307,15 +340,12 @@
     @pl.when(below & (c == 0))
     def _():
         for j in range(PANELS):
-            start(c >= 0, own_copies(j, own_source(j)))
-        for j in range(PANELS):
             own_load(j).start()
 
-    @pl.when(r == 1)
-    def _():
-        @pl.loop(0, LEAD)
-        def _(i):
-            cols_relay(1, i, x == 1)
+    @pl.loop(0, LEAD)
+    def _(i):
+        cols_relay(1, i, relays[1] & (i < lead))
+        cols_relay(0, i, relays[0] & (i < lead_left))
 
     for k in range(STARTS):
         diag_step(k)
@@ -340,14 +370,18 @@
         at = SLOTS * step + n
         i = at + lead
         pair = 2 * (at - LAG)
-        first = jnp.where(c == 1, pair, at)
+        first = jnp.where(c == 1, pair, at + lead_left)
         cols_relay(1, i, relays[1] & (i < CHUNKS))
         cols_relay(0, first, relays[0] & (first >= 0) & (first < CHUNKS))
         cols_relay(0, pair + 1, relays[0] & (c == 1) & (pair >= 0) & (pair < CHUNKS))
         if n % 2 == 1:
-            j = (at - LAG - 1) // 2
-
-            @pl.when(own_relays & (at > LAG) & (j < PANELS))
+            j = (at - own_lag) // 2
+
+            @pl.when(below & (c == 0) & (at >= own_lag) & (j < PANELS))
+            def _():
+                start(c >= 0, own_copies(j, own_source(j)))
+
+            @pl.when(own_relays & (at >= own_lag) & (j < PANELS))
             def _():
                 own_relay(j)
 
@@ -367,21 +401,26 @@
 
         half = width // 2
         own = split(own_ref[...])
-        for e in range(half, width + 1, half):
+
+        def panel(e):
             factor = split(w_ref[e - half : e, :e])
             panel_ref[:, e - half : e] = dot_split((own[0][:, :e], own[1][:, :e]), factor, 1)
 
-        for n in range(2):
-            @pl.when(jnp.logical_not(relays[n]) & ((c > 0) | (n == 1)))
-            def _():
-                @pl.loop(0, CHUNKS)
-                def _(i):
-                    cols_wait(n, i)
-
-        cols = split(cols_ref[...])
-        for e in range(half, width + 1, half):
-            factor = split(w_ref[e - half : e, :e])
-            other_ref[e - half : e, :] = dot_split(factor, (cols[0][:e, :], cols[1][:e, :]), 0)
+        def block_row(e):
+            for n in range(2):
+                @pl.when(jnp.logical_not(relays[n]) & ((c > 0) | (n == 1)))
+                def _():
+                    @pl.loop((e - half) // piece, e // piece)
+                    def _(i):
+                        cols_wait(n, i)
+
+            other_ref[e - half : e, :] = dot_split(split(w_ref[e - half : e, :e]), split(cols_ref[:e, :]), 0)
+
+        panel(half)
+        block_row(half)
+        rest_ref[...] = mine_ref[...] - dot_nn(panel_ref[:, :half], other_ref[:half, :])
+        panel(width)
+        block_row(width)
 
     @pl.when(corner)
     def _():
@@ -420,11 +459,11 @@
     return pl.pallas_call(
         panel_kernel,
         out_shape=(
-            square, jax.ShapeDtypeStruct(wide, jnp.float32), square,
+            square, jax.ShapeDtypeStruct(wide, jnp.float32), jax.ShapeDtypeStruct(wide, jnp.float32), square,
             jax.ShapeDtypeStruct((1, NB), jnp.float32),
         ),
-        in_specs=[pl.BlockSpec(memory_space=pl.ANY)],
-        out_specs=(VMEM,) * 4,
+        in_specs=[VMEM],
+        out_specs=(VMEM,) * 5,
         scratch_shapes=[
             pltpu.VMEM((width, width), jnp.float32), pltpu.VMEM(wide, jnp.float32),
             pltpu.VMEM((width, width), jnp.float32), pltpu.VMEM((width, width), jnp.float32),
@@ -433,12 +472,12 @@
             pltpu.VMEM((width, NB), jnp.float32),
             dma((4, tiles)), dma((tiles,)), dma((2, PANELS)), dma((PANELS,)), dma((4, CHUNKS)), dma((2, CHUNKS)),
         ],
-        compiler_params=pltpu.CompilerParams(collective_id=0, has_side_effects=True),
+        compiler_params=pltpu.CompilerParams(collective_id=0, has_side_effects=True, vmem_limit_bytes=28 << 20),
     )(mine)
 
 
 def per_device(mine):
-    panel, other, l, logdet = panel_step(mine)
+    panel, other, rest, l, logdet = panel_step(mine)
     width = mine.shape[0]
     across = pl.BlockSpec((width, width), lambda s: (0, s))
     whole = pl.BlockSpec((width, width), lambda s: (0, 0))
@@ -448,7 +487,8 @@
         out_shape=jax.ShapeDtypeStruct(mine.shape, jnp.float32),
         in_specs=[across, whole, across, whole],
         out_specs=across,
-    )(mine, panel, other, l)
+        compiler_params=pltpu.CompilerParams(vmem_limit_bytes=16 << 20),
+    )(rest, panel, other, l)
     return block, logdet[0, 0]
 
 

time: 61.6 us -> 54.8 us (0.89)
  the two profiles are of different devices: /device:TPU:28 before, /device:TPU:30 now
where the time goes in v2:
time: 54.8 us; the launch traced here: 54.6 us
  Pallas kernels  51.2 us (93%)
  between operations  1.81 us (3%)
  local copies, waits for them, and re-layouts  1.58 us (3%)
    pallas_call x1, Pallas kernels, panel_step(): pl.pallas_call(panel_kernel, out_shape=(square, jax.ShapeDtypeStruct(wide...  48.7 us
    pallas_call x1, Pallas kernels, per_device(): pl.pallas_call(update_kernel, grid=(mine.shape[1] // width,), out_shape=j...  2.51 us
    unnamed x2, local copies, waits for them, and re-layouts  1.58 us

profile of v2, /device:TPU:30, one launch (start us, length us, event | category | flops | bytes accessed | tf_op | source)
XLA Modules:
  0.0 54.6 jit_solution(9814305002638449722)
XLA Ops:
  0.6 0.0 copy-start
  0.6 1.6 %copy-done = f32[512,1024]{1,0:T(8,128)S(1)} copy-done((f32[512,1024]{1,0:T(8,128)S(1)}, f32[512,1024]{1,0:T(8,128)}, u32[]{:S(2)}) %copy-start) | copy-done | bytes 2097176
  2.2 48.7 %shard_map.30 = (f32[512,512]{1,0:T(8,128)S(1)}, f32[512,1024]{1,0:T(8,128)S(1)}, f32[512,1024]{1,0:T(8,128)S(1)}, f32[512,512]{1,0:T(8,128)S(1)}, f32[1,128]{1,0:T(1,128)S(1)}) custom-call(f32[512,1024]{1,0:T(8,128)S(1)} %copy-done), custom_call_target="tpu_custom_call" | custom-call | tf_op jit(solution)/shard_map/pallas_call | solution.py:459
  50.9 2.5 %shard_map.31 = f32[512,1024]{1,0:T(8,128)} custom-call(f32[512,1024]{1,0:T(8,128)S(1)} %get-tuple-element.7.rest_ref, f32[512,512]{1,0:T(8,128)S(1)} %get-tuple-element.8.panel_ref, f32[512,1024]{1,0:T(8,128)S(1)} %get-tuple-element.9.other_ref, f32[512,512]{1,0:T(8,128)S(1)} %get-tuple-element.10.l_ref), custom_call_target="tpu_custom_call" | custom-call | tf_op jit(solution)/shard_map/pallas_call | solution.py:484
Async XLA Ops:
  0.6 1.6 %copy-start = (f32[512,1024]{1,0:T(8,128)S(1)}, f32[512,1024]{1,0:T(8,128)}, u32[]{:S(2)}) copy-start(f32[512,1024]{1,0:T(8,128)} %mine_ref.1) | copy-start | bytes 6291460

commit v3 on v2

v3 whole, which is shorter than its diff:
```python
import functools

import jax
import jax.numpy as jnp
from jax import lax
from jax.experimental import pallas as pl
from jax.experimental.pallas import tpu as pltpu
from jax.sharding import PartitionSpec as P

MESH = pl.DeviceIdType.MESH
NB = 128
BAND = 32
CHUNKS = 32
LEAD = 8
AHEAD = 3
LAG = 6
LATE = 14
STARTS = 4
PANELS = 16
FIRST = 9
MIDDLE = 22
HOP = 3
LAST = 12
VMEM = pl.BlockSpec(memory_space=pltpu.VMEM)


def split(a):
    high = a.astype(jnp.bfloat16)
    return high, (a - high.astype(jnp.float32)).astype(jnp.bfloat16)


def dot_split(a, b, axis):
    def dot(u, v):
        return lax.dot_general(u, v, (((1,), (axis,)), ((), ())), preferred_element_type=jnp.float32)

    return dot(a[0], b[0]) + (dot(a[0], b[1]) + dot(a[1], b[0]))


def dot_nt(a, b):
    return dot_split(split(a), split(b), 1)


def dot_nn(a, b):
    return dot_split(split(a), split(b), 0)


def total(terms):
    while len(terms) > 1:
        terms = [a + b for a, b in zip(terms[::2], terms[1::2])]
    return terms[0]


def eliminate(left, right, base):
    sub = lax.broadcasted_iota(jnp.int32, (8, NB), 0)
    left, right = list(left), list(right)
    upper, inverse = [], []

    def row(x, t):
        return jnp.take_along_axis(x, jnp.full((8, NB), t, jnp.int32), axis=0)

    def column(x, t):
        return jnp.broadcast_to(x[:, t : t + 1], (8, NB))

    for p in range(0, len(left), 2):
        first = base + 8 * p
        rest = range(p + 2, len(left))
        cols = [[column(x, first + t) for x in left[p : p + 2]] for t in range(16)]
        mult = {g: [column(left[g], first + t) for t in range(16)] for g in rest}
        v, i = left[p : p + 2], right[p : p + 2]
        u_rows, i_rows, d_rows = list(v), list(i), [None, None]
        for t in range(16):
            at, s = t // 8, t % 8
            here = sub == s
            pivot = row(cols[t][at], s)
            if s:
                u_rows[at] = jnp.where(here, v[at], u_rows[at])
                i_rows[at] = jnp.where(here, i[at], i_rows[at])
                d_rows[at] = jnp.where(here, pivot, d_rows[at])
            else:
                u_rows[at], i_rows[at], d_rows[at] = v[at], i[at], pivot
            recip = 1.0 / pivot
            factor = [x * recip for x in cols[t]]
            factor[at] = jnp.where(here, -recip, factor[at])

            def step(pair):
                taken = row(pair[at], s)
                kept = [jnp.where(here, 0.0, x) if h == at else x for h, x in enumerate(pair)]
                return [x - f * taken for x, f in zip(kept, factor)]

            for w in range(t + 1, 16):
                cols[w] = step(cols[w])
            v, i = step(v), step(i)
        for h in range(2):
            scale = lax.rsqrt(d_rows[h])
            upper.append(u_rows[h] * scale)
            inverse.append(i_rows[h] * scale)
        v_rows = [row(v[t // 8], t % 8) for t in range(16)]
        i_rows = [row(i[t // 8], t % 8) for t in range(16)]
        for g in rest:
            left[g] = left[g] - total([mult[g][t] * v_rows[t] for t in range(16)])
            right[g] = right[g] - total([mult[g][t] * i_rows[t] for t in range(16)])
    return upper, inverse


def factor_block(a):
    lane = lax.broadcasted_iota(jnp.int32, (NB, NB), 1)
    sub = lax.broadcasted_iota(jnp.int32, (NB, NB), 0)
    left, right = a, (lane == sub).astype(jnp.float32)
    upper, inverse = [], []
    for base in range(0, NB, BAND):
        rows = [slice(8 * g, 8 * g + 8) for g in range(BAND // 8)]
        u, i = eliminate([left[x] for x in rows], [right[x] for x in rows], base)
        u, i = jnp.concatenate(u, 0), jnp.concatenate(i, 0)
        upper.append(u)
        inverse.append(i)
        if base + BAND < NB:
            change = dot_nn(u.T[base + BAND :, :], jnp.concatenate([u, i], 1))
            left, right = left[BAND:] - change[:, :NB], right[BAND:] - change[:, NB:]
    upper = jnp.where(lane >= sub, jnp.concatenate(upper, 0), 0.0)
    return upper, jnp.concatenate(inverse, 0)


def factor_all(a_ref, l_ref, w_ref, work, upper, inverse, arrive, leave):
    size = a_ref.shape[0]
    work[:NB, :NB] = a_ref[:NB, :NB]
    l_ref[...] = jnp.zeros_like(l_ref)
    w_ref[...] = jnp.zeros_like(w_ref)

    @pl.loop(0, size // NB)
    def _(step):
        span = pl.ds(pl.multiple_of(step * NB, NB), NB)
        r, w = factor_block(work[span, span])
        upper[...] = r
        inverse[...] = w
        w_ref[span, span] = inverse[...]
        l_ref[span, span] = upper[...].T
        for p in range(size // NB):

            @pl.when(step == p)
            def _():
                arrive(p)
                at = slice(p * NB, (p + 1) * NB)
                end = (p + 1) * NB
                if end < size:
                    below = work[end:, at] if p else a_ref[end:, at]
                    l_ref[end:, at] = dot_nt(below, inverse[...])
                    following = slice(end, end + NB)
                    work[end:, following] = a_ref[end:, following] - dot_nt(l_ref[end:, :end], l_ref[following, :end])
                if p:
                    inner = dot_nn(l_ref[at, : p * NB], w_ref[: p * NB, : p * NB])
                    w_ref[at, : p * NB] = -dot_nn(inverse[...], inner)
                    leave(p - 1)


def update_kernel(rest_ref, panel_ref, other_ref, l_ref, out_ref):
    r, c = lax.axis_index("row"), lax.axis_index("col")
    leading = (c == 0) & (pl.program_id(0) == 0)

    @pl.when(r == 0)
    def _():
        out_ref[...] = jnp.where(leading, l_ref[...], 0.0)

    @pl.when((r > 0) & leading)
    def _():
        out_ref[...] = panel_ref[...]

    @pl.when((r > 0) & jnp.logical_not(leading))
    def _():
        half = panel_ref.shape[1] // 2
        out_ref[...] = rest_ref[...] - dot_nn(panel_ref[:, half:], other_ref[half:, :])


def panel_kernel(mine_ref, panel_ref, other_ref, rest_ref, l_ref, logdet_ref,
                 own_ref, cols_ref, relay_ref, w_ref, diag_ref, work, upper, inverse,
                 diag_send, diag_recv, own_send, own_recv, cols_send, cols_recv, relay_send, relay_recv, w_send, w_recv):
    rows, columns = lax.axis_size("row"), lax.axis_size("col")
    r, c = lax.axis_index("row"), lax.axis_index("col")
    q, x = r // 2, r % 2
    other = r + 1 - 2 * x
    partner = c + 1 - 2 * (c % 2)
    odd = c % 2 == 1
    even = jnp.logical_not(odd)
    width = own_ref.shape[0]
    top = r == 0
    below = jnp.logical_not(top)
    corner = top & (c == 0)

    links = [
        ((r, partner), partner >= 0), ((other, c), odd),
        ((r - 2, c), odd & (r >= 2)), ((r + 2, c), odd & (r + 2 < rows)),
        ((r, c - 2), odd & (c >= 2)), ((r, c + 2), odd & (c + 2 < columns)),
        ((r + 1, partner), top & even), ((r + 2, partner), top & even),
        ((r - 1, partner), (r == 1) & odd), ((r - 2, partner), (r == 2) & odd),
    ]
    barrier = pltpu.get_barrier_semaphore()
    for device, exists in links:
        @pl.when(exists)
        def _():
            pl.semaphore_signal(barrier, inc=1, device_id=device, device_id_type=MESH)
    peers = sum(jnp.where(exists, 1, 0).astype(jnp.int32) for _, exists in links)
    pl.semaphore_wait(barrier, peers)

    def send(source, target, send_sem, recv_sem, device):
        return pltpu.make_async_remote_copy(
            src_ref=source, dst_ref=target, send_sem=send_sem, recv_sem=recv_sem,
            device_id=device, device_id_type=MESH,
        )

    def start(condition, copies):
        for exists, copy in copies:
            @pl.when(condition & exists)
            def _():
                copy.start()

    def drain(condition, copies):
        for exists, copy in copies:
            @pl.when(condition & exists)
            def _():
                copy.wait_send()

    side_row = jnp.where(x == 0, r + 1, r - 2)
    has_side = ((x == 0) & (q >= 1)) | (r == 3)

    tall = NB // STARTS
    tiles = [(pl.ds(i * tall, tall), pl.ds(0, NB)) for i in range(STARTS)]
    places = [(i, j) for j in range(width // NB) for i in range(j, width // NB) if i]
    tiles += [(pl.ds(i * NB, NB), pl.ds(j * NB, NB)) for i, j in places]

    def diag_load(k):
        return pltpu.make_async_copy(mine_ref.at[tiles[k]], diag_ref.at[tiles[k]], diag_recv.at[k])

    def diag_copies(k):
        tile = diag_ref.at[tiles[k]]

        def to(n, device):
            return send(tile, tile, diag_send.at[n, k], diag_recv.at[k], device)

        return [
            ((c == 1) & (x == 0) & (r + 2 < rows), to(0, (r + 2, c))),
            ((c == 1) & has_side, to(1, (side_row, c))),
            (c + 2 < columns, to(2, (r, c + 2))),
            (jnp.logical_not(top & (c == 1)), to(3, (r, c - 1))),
        ]

    def diag_first(k):
        return send(mine_ref.at[tiles[k]], diag_ref.at[tiles[k]], diag_send.at[0, k], diag_recv.at[k], (r, c + 1))

    def diag_relay(k):
        copies = diag_copies(k)
        copies[0][1].wait_recv()
        start(r >= 0, copies)

    def diag_wait(k):
        @pl.when(corner)
        def _():
            diag_load(k).wait()

        @pl.when(jnp.logical_not(corner))
        def _():
            diag_first(k).wait_recv()

    deep = width // PANELS

    def own_part(j):
        return own_ref.at[pl.ds(pl.multiple_of(j * deep, deep), deep), :]

    def own_source(j):
        return mine_ref.at[pl.ds(pl.multiple_of(j * deep, deep), deep), pl.ds(0, width)]

    def own_load(j):
        return pltpu.make_async_copy(own_source(j), own_part(j), own_recv.at[j])

    def own_first(j):
        return send(own_source(j), own_part(j), own_send.at[0, j], own_recv.at[j], (r, c + 1))

    def own_copies(j):
        part = own_part(j)

        def to(n, device):
            return send(part, part, own_send.at[n, j], own_recv.at[j], device)

        return [(c + 2 < columns, to(0, (r, c + 2))), (c > 1, to(1, (r, c - 1)))]

    def own_relay(j):
        copies = own_copies(j)
        copies[0][1].wait_recv()
        start(r >= 0, copies)

    piece = width // CHUNKS

    def cols_part(ref, half, i):
        return ref.at[pl.ds(pl.multiple_of(i * piece, piece), piece), pl.ds(half * width, width)]

    def routes(half):
        if half == 0:
            return [((x == 0) & (r + 2 < rows), (r + 2, c)), (has_side, (side_row, c))]
        return [((x == 1) & (r + 2 < rows), (r + 2, c)), ((x == 1) & (q >= 1), (r - 1, c))]

    def cols_first(half, i):
        return send(
            cols_part(mine_ref, half, i), cols_part(cols_ref, half, i), cols_send.at[half, i], cols_recv.at[half, i],
            (r + 2 - half, c),
        )

    def relay_first(half, i):
        return send(
            cols_part(mine_ref, half, i), cols_part(relay_ref, half, i), relay_send.at[half, i], relay_recv.at[half, i],
            (r + 2 - half, c + 1),
        )

    def cols_copies(half, i):
        part = cols_part(cols_ref, half, i)
        return [
            (exists, send(part, part, cols_send.at[2 * half + n, i], cols_recv.at[half, i], device))
            for n, (exists, device) in enumerate(routes(half))
        ]

    def relay_copies(half, i):
        part = cols_part(relay_ref, half, i)
        copies = [
            (exists, send(part, part, relay_send.at[3 * half + n, i], relay_recv.at[half, i], device))
            for n, (exists, device) in enumerate(routes(half))
        ]
        final = send(part, cols_part(cols_ref, half, i), relay_send.at[3 * half + 2, i], cols_recv.at[half, i], (r, c - 1))
        return copies + [(r >= 0, final)]

    def cols_relay(half, i):
        @pl.when((i >= 0) & (i < CHUNKS))
        def _():
            def pass_on(copies):
                copies[0][1].wait_recv()
                start(r >= 0, copies)

            if half == 0:
                @pl.when(c > 1)
                def _():
                    pass_on(relay_copies(0, i))
            else:
                pass_on(relay_copies(1, i))
            pass_on(cols_copies(half, i))

    def w_copy(p):
        part = w_ref.at[pl.ds(p * NB, NB), pl.ds(0, (p + 1) * NB)]
        return send(part, part, w_send.at[p], w_recv.at[p], (r, partner))

    steps = width // NB
    half = width // 2

    def log_det():
        here = lax.broadcasted_iota(jnp.int32, (NB, NB), 0) == lax.broadcasted_iota(jnp.int32, (NB, NB), 1)
        blocks = [slice(p * NB, (p + 1) * NB) for p in range(steps)]
        logs = sum(jnp.log(jnp.where(here, w_ref[at, at], 1.0)) for at in blocks)
        across = jnp.sum(logs, axis=0, keepdims=True)
        logdet_ref[...] = jnp.broadcast_to(-2.0 * jnp.sum(across, axis=1, keepdims=True), logdet_ref.shape)

    def panel(e, at=slice(None)):
        own = split(own_ref[at, :e])
        panel_ref[at, e - half : e] = dot_split(own, split(w_ref[e - half : e, :e]), 1)

    def block_row(e, at=slice(None)):
        other_ref[e - half : e, at] = dot_split(split(w_ref[e - half : e, :e]), split(cols_ref[:e, at]), 0)

    def update(at=slice(None)):
        rest_ref[:, at] = mine_ref[:, at] - dot_nn(panel_ref[:, :half], other_ref[:half, at])

    lower = [slice(i, i + half) for i in range(0, 2 * width, half)]

    def w_wait(first):
        for p in range(first, first + half // NB):
            w_copy(p).wait_recv()

    @pl.when(even)
    def _():
        @pl.when(corner)
        def _():
            for k in range(len(tiles)):
                diag_first(k).start()
            for k in range(len(tiles)):
                diag_load(k).start()

        @pl.when(top)
        def _():
            @pl.loop(0, CHUNKS)
            def _(i):
                relay_first(1, i).start()

                @pl.when(c > 0)
                def _():
                    relay_first(0, i).start()

        @pl.when(below & (c == 0))
        def _():
            for j in range(PANELS):
                own_first(j).start()
            for j in range(PANELS):
                own_load(j).start()

        for k in range(STARTS):
            diag_wait(k)

        def arrive(p):
            for k, (i, j) in enumerate(places):
                if (j == 0 and p == 0) or j == p + 1:
                    diag_wait(STARTS + k)

        factor_all(diag_ref, l_ref, w_ref, work, upper, inverse, arrive, lambda p: w_copy(p).start())
        log_det()

        @pl.when(below)
        def _():
            @pl.when(c == 0)
            def _():
                for j in range(PANELS):
                    own_load(j).wait()

            @pl.when(c > 0)
            def _():
                for j in range(PANELS):
                    own_first(j).wait_recv()

            panel(half)

        w_copy(steps - 1).start()

    @pl.when(odd)
    def _():
        for p in range(steps):
            if p * NB % half == 0 and half > NB:
                w_ref[p * NB : (p + 1) * NB, (p + 1) * NB : p * NB + half] = jnp.zeros((NB, half - NB), jnp.float32)

        @pl.when(top)
        def _():
            @pl.loop(0, CHUNKS)
            def _(i):
                cols_first(1, i).start()

                @pl.when(c > 1)
                def _():
                    cols_first(0, i).start()

        early = jnp.where(r == 1, LEAD, jnp.where(c > 1, AHEAD, 0))
        shift_a = jnp.where(r == 1, -LAG, 0) + jnp.where(c > 1, AHEAD, -LATE)
        shift_b = jnp.where(r == 1, LEAD, jnp.where(c > 1, AHEAD, 0)) - jnp.where(x == 0, LAG, 0)

        @pl.when(below)
        def _():
            @pl.loop(0, LEAD)
            def _(i):
                @pl.when(i < shift_b)
                def _():
                    cols_relay(1, i)

                @pl.when(i < shift_a)
                def _():
                    cols_relay(0, i)

        for k in range(STARTS):
            diag_relay(k)

        def turn(i):
            @pl.when(below)
            def _():
                cols_relay(1, i + shift_b)
                at = jnp.where(c > 1, i + shift_a, 2 * (i + shift_a))
                cols_relay(0, at)
                cols_relay(0, jnp.where(c > 1, CHUNKS, at + 1))
                j = i - jnp.minimum(FIRST + HOP * (c // 2), LAST)

                @pl.when((j >= 0) & (j < PANELS))
                def _():
                    own_relay(j)

        for k in range(len(places)):
            diag_relay(STARTS + k)
            turn(k)

        @pl.when(top & (c == 1))
        def _():
            @pl.loop(0, CHUNKS)
            def _(i):
                cols_first(0, i).start()

        @pl.loop(len(places), MIDDLE)
        def _(i):
            turn(i)

        w_wait(0)
        rows_of, left, right = lower[: width // half], lower[: width // half], lower[width // half :]
        work_items = [functools.partial(block_row, half, at) for at in right]
        work_items += [functools.partial(panel, half, rows_of[0]), None, None]
        work_items += [functools.partial(panel, half, at) for at in rows_of[1:]]
        work_items += [functools.partial(block_row, half, at) for at in left]
        work_items += [functools.partial(update, at) for at in right + left]
        for k, item in enumerate(work_items):
            turn(MIDDLE + k)
            if item is not None:
                pl.when(below)(item)

        @pl.loop(MIDDLE + len(work_items), CHUNKS + LAG + LATE)
        def _(i):
            turn(i)

        w_wait(half // NB)

        @pl.when(below)
        def _():
            panel(width)
            block_row(width)

        log_det()

    @pl.when(even & below)
    def _():
        def arrived(e):
            @pl.loop((e - half) // piece, e // piece)
            def _(i):
                cols_first(1, i).wait_recv()

                @pl.when(c > 0)
                def _():
                    cols_first(0, i).wait_recv()

        arrived(half)
        block_row(half)
        update()
        panel(width)
        arrived(width)
        block_row(width)

    @pl.when(even)
    def _():
        for p in range(steps):
            w_copy(p).wait_send()

        @pl.when(corner)
        def _():
            for k in range(len(tiles)):
                diag_first(k).wait_send()

        @pl.when(below & (c == 0))
        def _():
            for j in range(PANELS):
                own_first(j).wait_send()

        @pl.when(top)
        def _():
            @pl.loop(0, CHUNKS)
            def _(i):
                relay_first(1, i).wait_send()

                @pl.when(c > 0)
                def _():
                    relay_first(0, i).wait_send()

    @pl.when(odd)
    def _():
        for k in range(len(tiles)):
            drain(r >= 0, diag_copies(k))

        @pl.when(below)
        def _():
            @pl.loop(0, PANELS)
            def _(j):
                drain(r >= 0, own_copies(j))

        @pl.loop(0, CHUNKS)
        def _(i):
            @pl.when(top)
            def _():
                cols_first(1, i).wait_send()
                cols_first(0, i).wait_send()

            @pl.when(below)
            def _():
                for n in range(2):
                    drain(r >= 0, cols_copies(n, i))
                drain(r >= 0, relay_copies(1, i))

                @pl.when(c > 1)
                def _():
                    drain(r >= 0, relay_copies(0, i))


def panel_step(mine):
    width = mine.shape[0]
    square = jax.ShapeDtypeStruct((width, width), jnp.float32)
    wide = (width, 2 * width)
    dma = pltpu.SemaphoreType.DMA
    tiles = (width // NB) * (width // NB + 1) // 2 - 1 + STARTS
    return pl.pallas_call(
        panel_kernel,
        out_shape=(
            square, jax.ShapeDtypeStruct(wide, jnp.float32), jax.ShapeDtypeStruct(wide, jnp.float32), square,
            jax.ShapeDtypeStruct((1, NB), jnp.float32),
        ),
        in_specs=[VMEM],
        out_specs=(VMEM,) * 5,
        scratch_shapes=[
            pltpu.VMEM((width, width), jnp.float32), pltpu.VMEM(wide, jnp.float32), pltpu.VMEM(wide, jnp.float32),
            pltpu.VMEM((width, width), jnp.float32), pltpu.VMEM((width, width), jnp.float32),
            pltpu.VMEM((width, width), jnp.float32),
            pltpu.VMEM((NB, NB), jnp.float32), pltpu.VMEM((NB, NB), jnp.float32),
            dma((4, tiles)), dma((tiles,)), dma((2, PANELS)), dma((PANELS,)), dma((4, CHUNKS)), dma((2, CHUNKS)),
            dma((6, CHUNKS)), dma((2, CHUNKS)), dma((width // NB,)), dma((width // NB,)),
        ],
        compiler_params=pltpu.CompilerParams(collective_id=0, has_side_effects=True, vmem_limit_bytes=30 << 20),
    )(mine)


def per_device(mine):
    panel, other, rest, l, logdet = panel_step(mine)
    width = mine.shape[0]
    across = pl.BlockSpec((width, width), lambda s: (0, s))
    whole = pl.BlockSpec((width, width), lambda s: (0, 0))
    block = pl.pallas_call(
        update_kernel,
        grid=(mine.shape[1] // width,),
        out_shape=jax.ShapeDtypeStruct(mine.shape, jnp.float32),
        in_specs=[across, whole, across, whole],
        out_specs=across,
        compiler_params=pltpu.CompilerParams(vmem_limit_bytes=16 << 20),
    )(rest, panel, other, l)
    return block, logdet[0, 0]


def solution(mesh):
    return jax.shard_map(
        per_device, mesh=mesh, in_specs=(P("row", "col"),), out_specs=(P("row", "col"), P()), check_vma=False
    )
```

time: 54.8 us -> 52.1 us (0.951)
  the two profiles are of different devices: /device:TPU:30 before, /device:TPU:31 now
where the time goes in v3:
time: 52.1 us; the launch traced here: 51.9 us
  Pallas kernels  48.5 us (93%)
  between operations  1.81 us (3%)
  local copies, waits for them, and re-layouts  1.58 us (3%)
    pallas_call x1, Pallas kernels, panel_step(): pl.pallas_call(panel_kernel, out_shape=(square, jax.ShapeDtypeStruct(wide...  46 us
    pallas_call x1, Pallas kernels, per_device(): pl.pallas_call(update_kernel, grid=(mine.shape[1] // width,), out_shape=j...  2.51 us
    unnamed x2, local copies, waits for them, and re-layouts  1.58 us

profile of v3, /device:TPU:31, one launch (start us, length us, event | category | flops | bytes accessed | tf_op | source)
XLA Modules:
  0.0 51.9 jit_solution(15357106234033048407)
XLA Ops:
  0.6 0.0 copy-start
  0.6 1.6 %copy-done = f32[512,1024]{1,0:T(8,128)S(1)} copy-done((f32[512,1024]{1,0:T(8,128)S(1)}, f32[512,1024]{1,0:T(8,128)}, u32[]{:S(2)}) %copy-start) | copy-done | bytes 2097176
  2.2 46.0 %shard_map.30 = (f32[512,512]{1,0:T(8,128)S(1)}, f32[512,1024]{1,0:T(8,128)S(1)}, f32[512,1024]{1,0:T(8,128)S(1)}, f32[512,512]{1,0:T(8,128)S(1)}, f32[1,128]{1,0:T(1,128)S(1)}) custom-call(f32[512,1024]{1,0:T(8,128)S(1)} %copy-done), custom_call_target="tpu_custom_call" | custom-call | tf_op jit(solution)/shard_map/pallas_call | solution.py:590
  48.2 2.5 %shard_map.31 = f32[512,1024]{1,0:T(8,128)} custom-call(f32[512,1024]{1,0:T(8,128)S(1)} %get-tuple-element.7.rest_ref, f32[512,512]{1,0:T(8,128)S(1)} %get-tuple-element.8.panel_ref, f32[512,1024]{1,0:T(8,128)S(1)} %get-tuple-element.9.other_ref, f32[512,512]{1,0:T(8,128)S(1)} %get-tuple-element.10.l_ref), custom_call_target="tpu_custom_call" | custom-call | tf_op jit(solution)/shard_map/pallas_call | solution.py:615
Async XLA Ops:
  0.6 1.6 %copy-start = (f32[512,1024]{1,0:T(8,128)S(1)}, f32[512,1024]{1,0:T(8,128)}, u32[]{:S(2)}) copy-start(f32[512,1024]{1,0:T(8,128)} %mine_ref.1) | copy-start | bytes 6291460

commit v4 on v2

v4 whole, which is shorter than its diff:
```python
import functools

import jax
import jax.numpy as jnp
from jax import lax
from jax.experimental import pallas as pl
from jax.experimental.pallas import tpu as pltpu
from jax.sharding import PartitionSpec as P

MESH = pl.DeviceIdType.MESH
NB = 128
BAND = 32
CHUNKS = 32
PANELS = 16
HOPS = 2
FIRST = 2
DELAY = 3
LAST = 5
TURNS = (11, 17, 23, 26, 27, 28, 29)
WAIT = 3
MIDDLE = 22
VMEM = pl.BlockSpec(memory_space=pltpu.VMEM)


def split(a):
    high = a.astype(jnp.bfloat16)
    return high, (a - high.astype(jnp.float32)).astype(jnp.bfloat16)


def dot_split(a, b, axis):
    def dot(u, v):
        return lax.dot_general(u, v, (((1,), (axis,)), ((), ())), preferred_element_type=jnp.float32)

    return dot(a[0], b[0]) + (dot(a[0], b[1]) + dot(a[1], b[0]))


def dot_nt(a, b):
    return dot_split(split(a), split(b), 1)


def dot_nn(a, b):
    return dot_split(split(a), split(b), 0)


def total(terms):
    while len(terms) > 1:
        terms = [a + b for a, b in zip(terms[::2], terms[1::2])]
    return terms[0]


def eliminate(left, right, base):
    sub = lax.broadcasted_iota(jnp.int32, (8, NB), 0)
    left, right = list(left), list(right)
    upper, inverse = [], []

    def row(x, t):
        return jnp.take_along_axis(x, jnp.full((8, NB), t, jnp.int32), axis=0)

    def column(x, t):
        return jnp.broadcast_to(x[:, t : t + 1], (8, NB))

    for p in range(0, len(left), 2):
        first = base + 8 * p
        rest = range(p + 2, len(left))
        cols = [[column(x, first + t) for x in left[p : p + 2]] for t in range(16)]
        mult = {g: [column(left[g], first + t) for t in range(16)] for g in rest}
        v, i = left[p : p + 2], right[p : p + 2]
        u_rows, i_rows, d_rows = list(v), list(i), [None, None]
        for t in range(16):
            at, s = t // 8, t % 8
            here = sub == s
            pivot = row(cols[t][at], s)
            if s:
                u_rows[at] = jnp.where(here, v[at], u_rows[at])
                i_rows[at] = jnp.where(here, i[at], i_rows[at])
                d_rows[at] = jnp.where(here, pivot, d_rows[at])
            else:
                u_rows[at], i_rows[at], d_rows[at] = v[at], i[at], pivot
            recip = 1.0 / pivot
            factor = [x * recip for x in cols[t]]
            factor[at] = jnp.where(here, -recip, factor[at])

            def step(pair):
                taken = row(pair[at], s)
                kept = [jnp.where(here, 0.0, x) if h == at else x for h, x in enumerate(pair)]
                return [x - f * taken for x, f in zip(kept, factor)]

            for w in range(t + 1, 16):
                cols[w] = step(cols[w])
            v, i = step(v), step(i)
        for h in range(2):
            scale = lax.rsqrt(d_rows[h])
            upper.append(u_rows[h] * scale)
            inverse.append(i_rows[h] * scale)
        v_rows = [row(v[t // 8], t % 8) for t in range(16)]
        i_rows = [row(i[t // 8], t % 8) for t in range(16)]
        for g in rest:
            left[g] = left[g] - total([mult[g][t] * v_rows[t] for t in range(16)])
            right[g] = right[g] - total([mult[g][t] * i_rows[t] for t in range(16)])
    return upper, inverse


def factor_block(a):
    lane = lax.broadcasted_iota(jnp.int32, (NB, NB), 1)
    sub = lax.broadcasted_iota(jnp.int32, (NB, NB), 0)
    left, right = a, (lane == sub).astype(jnp.float32)
    upper, inverse = [], []
    for base in range(0, NB, BAND):
        rows = [slice(8 * g, 8 * g + 8) for g in range(BAND // 8)]
        u, i = eliminate([left[x] for x in rows], [right[x] for x in rows], base)
        u, i = jnp.concatenate(u, 0), jnp.concatenate(i, 0)
        upper.append(u)
        inverse.append(i)
        if base + BAND < NB:
            change = dot_nn(u.T[base + BAND :, :], jnp.concatenate([u, i], 1))
            left, right = left[BAND:] - change[:, :NB], right[BAND:] - change[:, NB:]
    upper = jnp.where(lane >= sub, jnp.concatenate(upper, 0), 0.0)
    return upper, jnp.concatenate(inverse, 0)


def factor_all(a_ref, l_ref, w_ref, work, upper, inverse, leave):
    size = w_ref.shape[0]
    work[:NB, :NB] = a_ref[:NB, :NB]
    l_ref[...] = jnp.zeros_like(l_ref)

    @pl.loop(0, size // NB)
    def _(step):
        span = pl.ds(pl.multiple_of(step * NB, NB), NB)
        r, w = factor_block(work[span, span])
        upper[...] = r
        inverse[...] = w
        w_ref[span, span] = inverse[...]
        l_ref[span, span] = upper[...].T
        for p in range(size // NB):

            @pl.when(step == p)
            def _():
                at = slice(p * NB, (p + 1) * NB)
                end = (p + 1) * NB
                if p:
                    leave(p - 1)
                if end < size:
                    below = work[end:, at] if p else a_ref[end:, at]
                    l_ref[end:, at] = dot_nt(below, inverse[...])
                    following = slice(end, end + NB)
                    work[end:, following] = a_ref[end:, following] - dot_nt(l_ref[end:, :end], l_ref[following, :end])
                if p:
                    inner = dot_nn(l_ref[at, : p * NB], w_ref[: p * NB, : p * NB])
                    w_ref[at, : p * NB] = -dot_nn(inverse[...], inner)


def update_kernel(rest_ref, panel_ref, other_ref, l_ref, out_ref):
    r, c = lax.axis_index("row"), lax.axis_index("col")
    leading = (c == 0) & (pl.program_id(0) == 0)

    @pl.when(r == 0)
    def _():
        out_ref[...] = jnp.where(leading, l_ref[...], 0.0)

    @pl.when((r > 0) & leading)
    def _():
        out_ref[...] = panel_ref[...]

    @pl.when((r > 0) & jnp.logical_not(leading))
    def _():
        half = panel_ref.shape[1] // 2
        out_ref[...] = rest_ref[...] - dot_nn(panel_ref[:, half:], other_ref[half:, :])


def panel_kernel(mine_ref, panel_ref, other_ref, rest_ref, l_ref, logdet_ref,
                 own_ref, cols_ref, w_ref, work, upper, inverse,
                 own_send, own_recv, cols_send, cols_recv, w_send, w_recv):
    rows, columns = lax.axis_size("row"), lax.axis_size("col")
    r, c = lax.axis_index("row"), lax.axis_index("col")
    q, x = r // 2, r % 2
    other = r + 1 - 2 * x
    partner = c + 1 - 2 * (c % 2)
    odd = c % 2 == 1
    even = jnp.logical_not(odd)
    width = own_ref.shape[0]
    top = r == 0
    below = jnp.logical_not(top)
    corner = top & (c == 0)

    links = [
        ((r, partner), partner >= 0), ((other, c), other >= 0),
        ((r - 2, c), r >= 2), ((r + 2, c), r + 2 < rows),
        ((r, c - 2), c >= 2), ((r, c + 2), c + 2 < columns),
    ]
    barrier = pltpu.get_barrier_semaphore()
    for device, exists in links:
        @pl.when(exists)
        def _():
            pl.semaphore_signal(barrier, inc=1, device_id=device, device_id_type=MESH)
    peers = sum(jnp.where(exists, 1, 0).astype(jnp.int32) for _, exists in links)
    pl.semaphore_wait(barrier, peers)

    def send(source, target, send_sem, recv_sem, device):
        return pltpu.make_async_remote_copy(
            src_ref=source, dst_ref=target, send_sem=send_sem, recv_sem=recv_sem,
            device_id=device, device_id_type=MESH,
        )

    def start(condition, copies):
        for exists, copy in copies:
            @pl.when(condition & exists)
            def _():
                copy.start()

    def drain(condition, copies):
        for exists, copy in copies:
            @pl.when(condition & exists)
            def _():
                copy.wait_send()

    side_row = jnp.where(x == 0, r + 1, r - 2)
    has_side = ((x == 0) & (q >= 1)) | (r == 3)

    steps = width // NB
    pieces = [(pl.ds(p * NB, NB), pl.ds(0, (p + 1) * NB)) for p in range(steps - 1)]
    pieces += [(pl.ds((steps - 1) * NB, NB), pl.ds(j * NB, NB)) for j in range(steps)]

    def w_first(m):
        part = w_ref.at[pieces[m]]
        return send(part, part, w_send.at[0, m], w_recv.at[m], (r, c + 1))

    def w_copies(m):
        part = w_ref.at[pieces[m]]

        def to(n, device):
            return send(part, part, w_send.at[n, m], w_recv.at[m], device)

        return [
            ((c == 1) & (x == 0) & (r + 2 < rows), to(0, (r + 2, c))),
            ((c == 1) & has_side, to(1, (side_row, c))),
            (c + 2 < columns, to(2, (r, c + 2))),
            (jnp.logical_not(top & (c == 1)), to(3, (r, c - 1))),
        ]

    def w_relay(m):
        copies = w_copies(m)
        copies[0][1].wait_recv()
        start(r >= 0, copies)

    deep = width // PANELS

    def own_part(j):
        return own_ref.at[pl.ds(pl.multiple_of(j * deep, deep), deep), :]

    def own_source(j):
        return mine_ref.at[pl.ds(pl.multiple_of(j * deep, deep), deep), pl.ds(0, width)]

    def own_load(j):
        return pltpu.make_async_copy(own_source(j), own_part(j), own_recv.at[j])

    def own_copies(j, source):
        def to(n, device):
            return send(source, own_part(j), own_send.at[n, j], own_recv.at[j], device)

        return [(c + 2 < columns, to(0, (r, c + 2))), (c >= 0, to(1, (r, c + 1)))]

    def own_wait(j):
        own_copies(j, own_part(j))[0][1].wait_recv()

    piece = width // CHUNKS

    def cols_part(ref, n, i):
        return ref.at[pl.ds(i * piece, piece), pl.ds(n * width, width)]

    def cols_copies(n, i, source):
        def to(m, device):
            return send(source, cols_part(cols_ref, n, i), cols_send.at[2 * n + m, i], cols_recv.at[n, i], device)

        return [((x == n) & (r + 2 < rows), to(0, (r + 2, c))), ((x == n) & (q >= 1) | (r == 3) & (n == 0), to(1, (sides[n], c)))]

    sides = [side_row, r - 1]
    relays = [(c > 0) & (((x == 0) & (q >= 1)) | (r == 3)), x == 1]

    def cols_first(n, i):
        source = cols_part(mine_ref, n, i)
        return send(source, cols_part(cols_ref, n, i), cols_send.at[2 * n, i], cols_recv.at[n, i], (r + 2 - n, c))

    def cols_wait(n, i):
        cols_first(n, i).wait_recv()

    def arrived(e):
        for n in range(2):
            @pl.when(jnp.logical_not(relays[n]) & ((c > 0) | (n == 1)))
            def _():
                for i in range((e - half) // piece, e // piece):
                    cols_wait(n, i)

    half = width // 2

    def log_det():
        here = lax.broadcasted_iota(jnp.int32, (NB, NB), 0) == lax.broadcasted_iota(jnp.int32, (NB, NB), 1)
        blocks = [slice(p * NB, (p + 1) * NB) for p in range(steps)]
        logs = sum(jnp.log(jnp.where(here, w_ref[at, at], 1.0)) for at in blocks)
        across = jnp.sum(logs, axis=0, keepdims=True)
        logdet_ref[...] = jnp.broadcast_to(-2.0 * jnp.sum(across, axis=1, keepdims=True), logdet_ref.shape)

    def panel(e, at=slice(None)):
        own = split(own_ref[at, :e])
        panel_ref[at, e - half : e] = dot_split(own, split(w_ref[e - half : e, :e]), 1)

    def block_row(e, at=slice(None)):
        other_ref[e - half : e, at] = dot_split(split(w_ref[e - half : e, :e]), split(cols_ref[:e, at]), 0)

    def update(at=slice(None)):
        rest_ref[:, at] = mine_ref[:, at] - dot_nn(panel_ref[:, :half], other_ref[:half, at])

    for p in range(steps):
        if p * NB % half == 0 and half > NB:
            w_ref[p * NB : (p + 1) * NB, (p + 1) * NB : p * NB + half] = jnp.zeros((NB, half - NB), jnp.float32)

    @pl.when(top)
    def _():
        for i in range(CHUNKS):
            cols_first(1, i).start()

            @pl.when(c > 0)
            def _():
                cols_first(0, i).start()

    @pl.when(below & (c == 0))
    def _():
        for j in range(PANELS):
            start(c >= 0, own_copies(j, own_source(j)))
        for j in range(PANELS):
            own_load(j).start()

    @pl.when(corner)
    def _():
        factor_all(mine_ref, l_ref, w_ref, work, upper, inverse, lambda p: w_first(p).start())
        log_det()
        for m in range(steps - 1, len(pieces)):
            w_first(m).start()

    @pl.when(top & odd)
    def _():
        for m in range(len(pieces)):
            w_relay(m)

    @pl.when(top & even & (c > 0))
    def _():
        for m in range(len(pieces)):
            w_first(m).wait_recv()

    first_half = half // NB
    patient = r == 1

    def w_arrive(first, last):
        @pl.when(even)
        def _():
            for m in range(first, last):
                w_first(m).wait_recv()

    def panel_arrive():
        @pl.when(c == 0)
        def _():
            for j in range(PANELS):
                own_load(j).wait()

        @pl.when(odd)
        def _():
            for j in range(PANELS):
                own_wait(j)

    lower = [slice(i, i + half) for i in range(0, 2 * width, half)]
    rows_of, right = lower[: width // half], lower[width // half :]
    items = [functools.partial(block_row, half, at) for at in right + rows_of]
    items += [functools.partial(panel, half, at) for at in rows_of]
    items += [functools.partial(update, at) for at in right + rows_of]

    @pl.when(below)
    def _():
        for i in range(CHUNKS):
            for n in range(2):
                @pl.when(relays[n])
                def _():
                    cols_wait(n, i)
                    start(c >= 0, cols_copies(n, i, cols_part(cols_ref, n, i)))

            for hop in range(1, HOPS + 1):
                j = i - min(FIRST + DELAY * (hop - 1), LAST)
                if 0 <= j < PANELS:
                    @pl.when(even & (c == 2 * hop if hop < HOPS else c >= 2 * hop))
                    def _():
                        own_wait(j)
                        start(c >= 0, own_copies(j, own_part(j)))

            for m, turn in enumerate(TURNS):
                for late, plane in ((0, c == 1), (WAIT, c > 1)):
                    if min(turn + late, CHUNKS - 1) == i:
                        @pl.when(odd & plane & jnp.logical_not(patient))
                        def _():
                            w_relay(m)

            if i == MIDDLE:
                @pl.when(jnp.logical_not(patient))
                def _():
                    w_arrive(0, first_half)
                    panel_arrive()
                    arrived(half)

            if MIDDLE <= i < MIDDLE + len(items):
                pl.when(jnp.logical_not(patient))(items[i - MIDDLE])

        @pl.when(patient)
        def _():
            @pl.when(odd)
            def _():
                for m in range(len(pieces)):
                    w_relay(m)

            w_arrive(0, first_half)
            panel_arrive()
            arrived(half)
            block_row(half)
            panel(half)
            update()

        w_arrive(first_half, len(pieces))
        panel(width)
        arrived(width)
        block_row(width)

    @pl.when(jnp.logical_not(corner))
    def _():
        log_det()

    @pl.when(corner)
    def _():
        for m in range(len(pieces)):
            w_first(m).wait_send()

    for m in range(len(pieces)):
        drain(odd, w_copies(m))

    @pl.when(below & even)
    def _():
        for j in range(PANELS):
            drain(c >= 0, own_copies(j, own_part(j)))

    for i in range(CHUNKS):
        @pl.when(top)
        def _():
            cols_first(1, i).wait_send()

            @pl.when(c > 0)
            def _():
                cols_first(0, i).wait_send()

        for n in range(2):
            drain(below & relays[n], cols_copies(n, i, cols_part(cols_ref, n, i)))


def panel_step(mine):
    width = mine.shape[0]
    square = jax.ShapeDtypeStruct((width, width), jnp.float32)
    wide = (width, 2 * width)
    dma = pltpu.SemaphoreType.DMA
    pieces = 2 * (width // NB) - 1
    return pl.pallas_call(
        panel_kernel,
        out_shape=(
            square, jax.ShapeDtypeStruct(wide, jnp.float32), jax.ShapeDtypeStruct(wide, jnp.float32), square,
            jax.ShapeDtypeStruct((1, NB), jnp.float32),
        ),
        in_specs=[VMEM],
        out_specs=(VMEM,) * 5,
        scratch_shapes=[
            pltpu.VMEM((width, width), jnp.float32), pltpu.VMEM(wide, jnp.float32),
            pltpu.VMEM((width, width), jnp.float32), pltpu.VMEM((width, width), jnp.float32),
            pltpu.VMEM((NB, NB), jnp.float32), pltpu.VMEM((NB, NB), jnp.float32),
            dma((2, PANELS)), dma((PANELS,)), dma((4, CHUNKS)), dma((2, CHUNKS)), dma((4, pieces)), dma((pieces,)),
        ],
        compiler_params=pltpu.CompilerParams(collective_id=0, has_side_effects=True, vmem_limit_bytes=30 << 20),
    )(mine)


def per_device(mine):
    panel, other, rest, l, logdet = panel_step(mine)
    width = mine.shape[0]
    across = pl.BlockSpec((width, width), lambda s: (0, s))
    whole = pl.BlockSpec((width, width), lambda s: (0, 0))
    block = pl.pallas_call(
        update_kernel,
        grid=(mine.shape[1] // width,),
        out_shape=jax.ShapeDtypeStruct(mine.shape, jnp.float32),
        in_specs=[across, whole, across, whole],
        out_specs=across,
        compiler_params=pltpu.CompilerParams(vmem_limit_bytes=16 << 20),
    )(rest, panel, other, l)
    return block, logdet[0, 0]


def solution(mesh):
    return jax.shard_map(
        per_device, mesh=mesh, in_specs=(P("row", "col"),), out_specs=(P("row", "col"), P()), check_vma=False
    )
```

time: 54.8 us -> 52 us (0.949)
  the two profiles are of different devices: /device:TPU:30 before, /device:TPU:25 now
where the time goes in v4:
time: 52 us; the launch traced here: 51.7 us
  Pallas kernels  48.3 us (93%)
  between operations  1.81 us (3%)
  local copies, waits for them, and re-layouts  1.58 us (3%)
    pallas_call x1, Pallas kernels, panel_step(): pl.pallas_call(panel_kernel, out_shape=(square, jax.ShapeDtypeStruct(wide...  45.8 us
    pallas_call x1, Pallas kernels, per_device(): pl.pallas_call(update_kernel, grid=(mine.shape[1] // width,), out_shape=j...  2.51 us
    unnamed x2, local copies, waits for them, and re-layouts  1.58 us

profile of v4, /device:TPU:25, one launch (start us, length us, event | category | flops | bytes accessed | tf_op | source)
XLA Modules:
  0.0 51.7 jit_solution(17748138490072670656)
XLA Ops:
  0.6 0.0 copy-start
  0.6 1.6 %copy-done = f32[512,1024]{1,0:T(8,128)S(1)} copy-done((f32[512,1024]{1,0:T(8,128)S(1)}, f32[512,1024]{1,0:T(8,128)}, u32[]{:S(2)}) %copy-start) | copy-done | bytes 2097176
  2.2 45.8 %shard_map.30 = (f32[512,512]{1,0:T(8,128)S(1)}, f32[512,1024]{1,0:T(8,128)S(1)}, f32[512,1024]{1,0:T(8,128)S(1)}, f32[512,512]{1,0:T(8,128)S(1)}, f32[1,128]{1,0:T(1,128)S(1)}) custom-call(f32[512,1024]{1,0:T(8,128)S(1)} %copy-done), custom_call_target="tpu_custom_call" | custom-call | tf_op jit(solution)/shard_map/pallas_call | solution.py:464
  48.0 2.5 %shard_map.31 = f32[512,1024]{1,0:T(8,128)} custom-call(f32[512,1024]{1,0:T(8,128)S(1)} %get-tuple-element.7.rest_ref, f32[512,512]{1,0:T(8,128)S(1)} %get-tuple-element.8.panel_ref, f32[512,1024]{1,0:T(8,128)S(1)} %get-tuple-element.9.other_ref, f32[512,512]{1,0:T(8,128)S(1)} %get-tuple-element.10.l_ref), custom_call_target="tpu_custom_call" | custom-call | tf_op jit(solution)/shard_map/pallas_call | solution.py:487
Async XLA Ops:
  0.6 1.6 %copy-start = (f32[512,1024]{1,0:T(8,128)S(1)}, f32[512,1024]{1,0:T(8,128)}, u32[]{:S(2)}) copy-start(f32[512,1024]{1,0:T(8,128)} %mine_ref.1) | copy-start | bytes 6291460

commit v5 on v4

--- a/solution.py
+++ b/solution.py
@@ -207,12 +207,6 @@
             def _():
                 copy.start()
 
-    def drain(condition, copies):
-        for exists, copy in copies:
-            @pl.when(condition & exists)
-            def _():
-                copy.wait_send()
-
     side_row = jnp.where(x == 0, r + 1, r - 2)
     has_side = ((x == 0) & (q >= 1)) | (r == 3)
 
@@ -222,13 +216,13 @@
 
     def w_first(m):
         part = w_ref.at[pieces[m]]
-        return send(part, part, w_send.at[0, m], w_recv.at[m], (r, c + 1))
+        return send(part, part, w_send.at[0], w_recv.at[m], (r, c + 1))
 
     def w_copies(m):
         part = w_ref.at[pieces[m]]
 
         def to(n, device):
-            return send(part, part, w_send.at[n, m], w_recv.at[m], device)
+            return send(part, part, w_send.at[n], w_recv.at[m], device)
 
         return [
             ((c == 1) & (x == 0) & (r + 2 < rows), to(0, (r + 2, c))),
@@ -255,7 +249,7 @@
 
     def own_copies(j, source):
         def to(n, device):
-            return send(source, own_part(j), own_send.at[n, j], own_recv.at[j], device)
+            return send(source, own_part(j), own_send.at[n], own_recv.at[j], device)
 
         return [(c + 2 < columns, to(0, (r, c + 2))), (c >= 0, to(1, (r, c + 1)))]
 
@@ -269,7 +263,7 @@
 
     def cols_copies(n, i, source):
         def to(m, device):
-            return send(source, cols_part(cols_ref, n, i), cols_send.at[2 * n + m, i], cols_recv.at[n, i], device)
+            return send(source, cols_part(cols_ref, n, i), cols_send.at[2 * n + m], cols_recv.at[n, i], device)
 
         return [((x == n) & (r + 2 < rows), to(0, (r + 2, c))), ((x == n) & (q >= 1) | (r == 3) & (n == 0), to(1, (sides[n], c)))]
 
@@ -278,7 +272,7 @@
 
     def cols_first(n, i):
         source = cols_part(mine_ref, n, i)
-        return send(source, cols_part(cols_ref, n, i), cols_send.at[2 * n, i], cols_recv.at[n, i], (r + 2 - n, c))
+        return send(source, cols_part(cols_ref, n, i), cols_send.at[2 * n], cols_recv.at[n, i], (r + 2 - n, c))
 
     def cols_wait(n, i):
         cols_first(n, i).wait_recv()
@@ -348,6 +342,7 @@
 
     first_half = half // NB
     patient = r == 1
+    between = (x == 1) & (r + 2 >= rows)
 
     def w_arrive(first, last):
         @pl.when(even)
@@ -397,22 +392,22 @@
                             w_relay(m)
 
             if i == MIDDLE:
-                @pl.when(jnp.logical_not(patient))
+                @pl.when(between)
                 def _():
                     w_arrive(0, first_half)
                     panel_arrive()
                     arrived(half)
 
             if MIDDLE <= i < MIDDLE + len(items):
-                pl.when(jnp.logical_not(patient))(items[i - MIDDLE])
-
-        @pl.when(patient)
-        def _():
-            @pl.when(odd)
-            def _():
-                for m in range(len(pieces)):
-                    w_relay(m)
-
+                pl.when(between)(items[i - MIDDLE])
+
+        @pl.when(patient & odd)
+        def _():
+            for m in range(len(pieces)):
+                w_relay(m)
+
+        @pl.when(jnp.logical_not(between))
+        def _():
             w_arrive(0, first_half)
             panel_arrive()
             arrived(half)
@@ -429,30 +424,22 @@
     def _():
         log_det()
 
-    @pl.when(corner)
-    def _():
-        for m in range(len(pieces)):
-            w_first(m).wait_send()
-
-    for m in range(len(pieces)):
-        drain(odd, w_copies(m))
-
-    @pl.when(below & even)
-    def _():
-        for j in range(PANELS):
-            drain(c >= 0, own_copies(j, own_part(j)))
-
-    for i in range(CHUNKS):
-        @pl.when(top)
-        def _():
-            cols_first(1, i).wait_send()
-
-            @pl.when(c > 0)
-            def _():
-                cols_first(0, i).wait_send()
-
-        for n in range(2):
-            drain(below & relays[n], cols_copies(n, i, cols_part(cols_ref, n, i)))
+    def sent(condition, part, sem):
+        @pl.when(condition)
+        def _():
+            send(part, part, sem, w_recv.at[0], (r, partner)).wait_send()
+
+    inverse_part = cols_ref.at[pl.ds(0, (steps + 1) * NB // 4), :]
+    sent(corner, inverse_part, w_send.at[0])
+    for n, (exists, _) in enumerate(w_copies(0)):
+        sent(odd & exists, inverse_part, w_send.at[n])
+    for n, (exists, _) in enumerate(own_copies(0, own_part(0))):
+        sent(below & even & exists, own_ref, own_send.at[n])
+    for n in range(2):
+        part = cols_ref.at[:, pl.ds(n * width, width)]
+        sent(top & ((c > 0) | (n == 1)), part, cols_send.at[2 * n])
+        for m, (exists, _) in enumerate(cols_copies(n, 0, cols_part(cols_ref, n, 0))):
+            sent(below & relays[n] & exists, part, cols_send.at[2 * n + m])
 
 
 def panel_step(mine):
@@ -473,7 +460,7 @@
             pltpu.VMEM((width, width), jnp.float32), pltpu.VMEM(wide, jnp.float32),
             pltpu.VMEM((width, width), jnp.float32), pltpu.VMEM((width, width), jnp.float32),
             pltpu.VMEM((NB, NB), jnp.float32), pltpu.VMEM((NB, NB), jnp.float32),
-            dma((2, PANELS)), dma((PANELS,)), dma((4, CHUNKS)), dma((2, CHUNKS)), dma((4, pieces)), dma((pieces,)),
+            dma((2,)), dma((PANELS,)), dma((4,)), dma((2, CHUNKS)), dma((4,)), dma((pieces,)),
         ],
         compiler_params=pltpu.CompilerParams(collective_id=0, has_side_effects=True, vmem_limit_bytes=30 << 20),
     )(mine)

time: 52 us -> 48 us (0.923)
  Pallas kernels: 48.3 us -> 44.3 us
    pallas_call x1, Pallas kernels: 45.8 us -> 41.8 us  [panel_step(): pl.pallas_call(panel_kernel, out_shape=(square, jax.ShapeDtypeStruct(wide...]
where the time goes in v5:
time: 48 us; the launch traced here: 47.7 us
  Pallas kernels  44.3 us (92%)
  between operations  1.81 us (4%)
  local copies, waits for them, and re-layouts  1.58 us (3%)
    pallas_call x1, Pallas kernels, panel_step(): pl.pallas_call(panel_kernel, out_shape=(square, jax.ShapeDtypeStruct(wide...  41.8 us
    pallas_call x1, Pallas kernels, per_device(): pl.pallas_call(update_kernel, grid=(mine.shape[1] // width,), out_shape=j...  2.51 us
    unnamed x2, local copies, waits for them, and re-layouts  1.58 us

profile of v5, /device:TPU:25, one launch (start us, length us, event | category | flops | bytes accessed | tf_op | source)
XLA Modules:
  0.0 47.7 jit_solution(8752593577471939082)
XLA Ops:
  0.6 0.0 copy-start
  0.6 1.6 %copy-done = f32[512,1024]{1,0:T(8,128)S(1)} copy-done((f32[512,1024]{1,0:T(8,128)S(1)}, f32[512,1024]{1,0:T(8,128)}, u32[]{:S(2)}) %copy-start) | copy-done | bytes 2097176
  2.2 41.8 %shard_map.30 = (f32[512,512]{1,0:T(8,128)S(1)}, f32[512,1024]{1,0:T(8,128)S(1)}, f32[512,1024]{1,0:T(8,128)S(1)}, f32[512,512]{1,0:T(8,128)S(1)}, f32[1,128]{1,0:T(1,128)S(1)}) custom-call(f32[512,1024]{1,0:T(8,128)S(1)} %copy-done), custom_call_target="tpu_custom_call" | custom-call | tf_op jit(solution)/shard_map/pallas_call | solution.py:451
  44.1 2.5 %shard_map.31 = f32[512,1024]{1,0:T(8,128)} custom-call(f32[512,1024]{1,0:T(8,128)S(1)} %get-tuple-element.7.rest_ref, f32[512,512]{1,0:T(8,128)S(1)} %get-tuple-element.8.panel_ref, f32[512,1024]{1,0:T(8,128)S(1)} %get-tuple-element.9.other_ref, f32[512,512]{1,0:T(8,128)S(1)} %get-tuple-element.10.l_ref), custom_call_target="tpu_custom_call" | custom-call | tf_op jit(solution)/shard_map/pallas_call | solution.py:474
Async XLA Ops:
  0.6 1.6 %copy-start = (f32[512,1024]{1,0:T(8,128)S(1)}, f32[512,1024]{1,0:T(8,128)}, u32[]{:S(2)}) copy-start(f32[512,1024]{1,0:T(8,128)} %mine_ref.1) | copy-start | bytes 6291460

commit v6 on v5

--- a/solution.py
+++ b/solution.py
@@ -16,7 +16,8 @@
 FIRST = 2
 DELAY = 3
 LAST = 5
-TURNS = (11, 17, 23, 26, 27, 28, 29)
+TURNS = (10, 11, 15, 16, 17, 18, 21, 21, 22, 22, 23, 24, 24, 25, 25, 26, 26, 27, 27, 28)
+FOLLOW = 12
 WAIT = 3
 MIDDLE = 22
 VMEM = pl.BlockSpec(memory_space=pltpu.VMEM)
@@ -211,8 +212,13 @@
     has_side = ((x == 0) & (q >= 1)) | (r == 3)
 
     steps = width // NB
-    pieces = [(pl.ds(p * NB, NB), pl.ds(0, (p + 1) * NB)) for p in range(steps - 1)]
-    pieces += [(pl.ds((steps - 1) * NB, NB), pl.ds(j * NB, NB)) for j in range(steps)]
+    tall = NB // 2
+    pieces = [
+        (pl.ds(p * NB + h * tall, tall), pl.ds(j * NB, NB)) for p in range(steps) for j in range(p + 1) for h in range(2)
+    ]
+
+    def row_pieces(p):
+        return range(p * (p + 1), (p + 1) * (p + 2))
 
     def w_first(m):
         part = w_ref.at[pieces[m]]
@@ -323,12 +329,15 @@
         for j in range(PANELS):
             own_load(j).start()
 
+    def w_leave(p):
+        for m in row_pieces(p):
+            w_first(m).start()
+
     @pl.when(corner)
     def _():
-        factor_all(mine_ref, l_ref, w_ref, work, upper, inverse, lambda p: w_first(p).start())
+        factor_all(mine_ref, l_ref, w_ref, work, upper, inverse, w_leave)
         log_det()
-        for m in range(steps - 1, len(pieces)):
-            w_first(m).start()
+        w_leave(steps - 1)
 
     @pl.when(top & odd)
     def _():
@@ -340,7 +349,7 @@
         for m in range(len(pieces)):
             w_first(m).wait_recv()
 
-    first_half = half // NB
+    first_half = row_pieces(half // NB)[0]
     patient = r == 1
     between = (x == 1) & (r + 2 >= rows)
 
@@ -386,7 +395,7 @@
 
             for m, turn in enumerate(TURNS):
                 for late, plane in ((0, c == 1), (WAIT, c > 1)):
-                    if min(turn + late, CHUNKS - 1) == i:
+                    if turn + late == i and (late == 0 or m < FOLLOW):
                         @pl.when(odd & plane & jnp.logical_not(patient))
                         def _():
                             w_relay(m)
@@ -415,10 +424,19 @@
             panel(half)
             update()
 
+        @pl.when(odd & (c > 1) & jnp.logical_not(patient))
+        def _():
+            for m in range(FOLLOW, len(pieces)):
+                w_relay(m)
+
         w_arrive(first_half, len(pieces))
         panel(width)
-        arrived(width)
-        block_row(width)
+        for n in range(2):
+            @pl.when(x == n)
+            def _():
+                block_row(width, slice(n * width, (n + 1) * width))
+                arrived(width)
+                block_row(width, slice((1 - n) * width, (2 - n) * width))
 
     @pl.when(jnp.logical_not(corner))
     def _():
@@ -447,7 +465,7 @@
     square = jax.ShapeDtypeStruct((width, width), jnp.float32)
     wide = (width, 2 * width)
     dma = pltpu.SemaphoreType.DMA
-    pieces = 2 * (width // NB) - 1
+    pieces = (width // NB) * (width // NB + 1)
     return pl.pallas_call(
         panel_kernel,
         out_shape=(

time: 48 us -> 45.9 us (0.956)
  Pallas kernels: 44.3 us -> 42.3 us
    pallas_call x1, Pallas kernels: 41.8 us -> 39.8 us  [panel_step(): pl.pallas_call(panel_kernel, out_shape=(square, jax.ShapeDtypeStruct(wide...]
where the time goes in v6:
time: 45.9 us; the launch traced here: 45.7 us
  Pallas kernels  42.3 us (92%)
  between operations  1.81 us (4%)
  local copies, waits for them, and re-layouts  1.58 us (3%)
    pallas_call x1, Pallas kernels, panel_step(): pl.pallas_call(panel_kernel, out_shape=(square, jax.ShapeDtypeStruct(wide...  39.8 us
    pallas_call x1, Pallas kernels, per_device(): pl.pallas_call(update_kernel, grid=(mine.shape[1] // width,), out_shape=j...  2.51 us
    unnamed x2, local copies, waits for them, and re-layouts  1.58 us

profile of v6, /device:TPU:25, one launch (start us, length us, event | category | flops | bytes accessed | tf_op | source)
XLA Modules:
  0.0 45.7 jit_solution(1888192949571054797)
XLA Ops:
  0.6 0.0 copy-start
  0.6 1.6 %copy-done = f32[512,1024]{1,0:T(8,128)S(1)} copy-done((f32[512,1024]{1,0:T(8,128)S(1)}, f32[512,1024]{1,0:T(8,128)}, u32[]{:S(2)}) %copy-start) | copy-done | bytes 2097176
  2.2 39.8 %shard_map.30 = (f32[512,512]{1,0:T(8,128)S(1)}, f32[512,1024]{1,0:T(8,128)S(1)}, f32[512,1024]{1,0:T(8,128)S(1)}, f32[512,512]{1,0:T(8,128)S(1)}, f32[1,128]{1,0:T(1,128)S(1)}) custom-call(f32[512,1024]{1,0:T(8,128)S(1)} %copy-done), custom_call_target="tpu_custom_call" | custom-call | tf_op jit(solution)/shard_map/pallas_call | solution.py:469
  42.1 2.5 %shard_map.31 = f32[512,1024]{1,0:T(8,128)} custom-call(f32[512,1024]{1,0:T(8,128)S(1)} %get-tuple-element.7.rest_ref, f32[512,512]{1,0:T(8,128)S(1)} %get-tuple-element.8.panel_ref, f32[512,1024]{1,0:T(8,128)S(1)} %get-tuple-element.9.other_ref, f32[512,512]{1,0:T(8,128)S(1)} %get-tuple-element.10.l_ref), custom_call_target="tpu_custom_call" | custom-call | tf_op jit(solution)/shard_map/pallas_call | solution.py:492
Async XLA Ops:
  0.6 1.6 %copy-start = (f32[512,1024]{1,0:T(8,128)S(1)}, f32[512,1024]{1,0:T(8,128)}, u32[]{:S(2)}) copy-start(f32[512,1024]{1,0:T(8,128)} %mine_ref.1) | copy-start | bytes 6291460

commit v7 on v6

--- a/solution.py
+++ b/solution.py
@@ -150,27 +150,9 @@
                     w_ref[at, : p * NB] = -dot_nn(inverse[...], inner)
 
 
-def update_kernel(rest_ref, panel_ref, other_ref, l_ref, out_ref):
-    r, c = lax.axis_index("row"), lax.axis_index("col")
-    leading = (c == 0) & (pl.program_id(0) == 0)
-
-    @pl.when(r == 0)
-    def _():
-        out_ref[...] = jnp.where(leading, l_ref[...], 0.0)
-
-    @pl.when((r > 0) & leading)
-    def _():
-        out_ref[...] = panel_ref[...]
-
-    @pl.when((r > 0) & jnp.logical_not(leading))
-    def _():
-        half = panel_ref.shape[1] // 2
-        out_ref[...] = rest_ref[...] - dot_nn(panel_ref[:, half:], other_ref[half:, :])
-
-
-def panel_kernel(mine_ref, panel_ref, other_ref, rest_ref, l_ref, logdet_ref,
-                 own_ref, cols_ref, w_ref, work, upper, inverse,
-                 own_send, own_recv, cols_send, cols_recv, w_send, w_recv):
+def panel_kernel(mine_ref, rest_ref, logdet_ref,
+                 panel_ref, other_ref, l_ref, own_ref, cols_ref, w_ref, work, upper, inverse,
+                 own_send, own_recv, cols_send, cols_recv, w_send, w_recv, load_sem):
     rows, columns = lax.axis_size("row"), lax.axis_size("col")
     r, c = lax.axis_index("row"), lax.axis_index("col")
     q, x = r // 2, r % 2
@@ -306,12 +288,24 @@
     def block_row(e, at=slice(None)):
         other_ref[e - half : e, at] = dot_split(split(w_ref[e - half : e, :e]), split(cols_ref[:e, at]), 0)
 
+    mine_load = pltpu.make_async_copy(mine_ref, rest_ref, load_sem)
+
     def update(at=slice(None)):
-        rest_ref[:, at] = mine_ref[:, at] - dot_nn(panel_ref[:, :half], other_ref[:half, at])
+        rest_ref[:, at] = rest_ref[:, at] - dot_nn(panel_ref[:, :half], other_ref[:half, at])
+
+    def finish(at):
+        block_row(width, at)
+        rest_ref[:, at] = rest_ref[:, at] - dot_nn(panel_ref[:, half:], other_ref[half:, at])
 
     for p in range(steps):
         if p * NB % half == 0 and half > NB:
             w_ref[p * NB : (p + 1) * NB, (p + 1) * NB : p * NB + half] = jnp.zeros((NB, half - NB), jnp.float32)
+
+    diagonal_load = pltpu.make_async_copy(mine_ref.at[:, pl.ds(0, width)], own_ref, load_sem)
+
+    @pl.when(corner)
+    def _():
+        diagonal_load.start()
 
     @pl.when(top)
     def _():
@@ -329,13 +323,18 @@
         for j in range(PANELS):
             own_load(j).start()
 
+    @pl.when(below)
+    def _():
+        mine_load.start()
+
     def w_leave(p):
         for m in row_pieces(p):
             w_first(m).start()
 
     @pl.when(corner)
     def _():
-        factor_all(mine_ref, l_ref, w_ref, work, upper, inverse, w_leave)
+        diagonal_load.wait()
+        factor_all(own_ref, l_ref, w_ref, work, upper, inverse, w_leave)
         log_det()
         w_leave(steps - 1)
 
@@ -360,6 +359,8 @@
                 w_first(m).wait_recv()
 
     def panel_arrive():
+        mine_load.wait()
+
         @pl.when(c == 0)
         def _():
             for j in range(PANELS):
@@ -434,9 +435,21 @@
         for n in range(2):
             @pl.when(x == n)
             def _():
-                block_row(width, slice(n * width, (n + 1) * width))
+                finish(slice(n * width, (n + 1) * width))
                 arrived(width)
-                block_row(width, slice((1 - n) * width, (2 - n) * width))
+                finish(slice((1 - n) * width, (2 - n) * width))
+
+        @pl.when(c == 0)
+        def _():
+            rest_ref[:, :width] = panel_ref[...]
+
+    @pl.when(top)
+    def _():
+        rest_ref[...] = jnp.zeros_like(rest_ref)
+
+    @pl.when(corner)
+    def _():
+        rest_ref[:, :width] = l_ref[...]
 
     @pl.when(jnp.logical_not(corner))
     def _():
@@ -468,35 +481,22 @@
     pieces = (width // NB) * (width // NB + 1)
     return pl.pallas_call(
         panel_kernel,
-        out_shape=(
-            square, jax.ShapeDtypeStruct(wide, jnp.float32), jax.ShapeDtypeStruct(wide, jnp.float32), square,
-            jax.ShapeDtypeStruct((1, NB), jnp.float32),
-        ),
-        in_specs=[VMEM],
-        out_specs=(VMEM,) * 5,
+        out_shape=(jax.ShapeDtypeStruct(wide, jnp.float32), jax.ShapeDtypeStruct((1, NB), jnp.float32)),
+        in_specs=[pl.BlockSpec(memory_space=pltpu.HBM)],
+        out_specs=(VMEM,) * 2,
         scratch_shapes=[
+            pltpu.VMEM((width, width), jnp.float32), pltpu.VMEM(wide, jnp.float32), pltpu.VMEM((width, width), jnp.float32),
             pltpu.VMEM((width, width), jnp.float32), pltpu.VMEM(wide, jnp.float32),
             pltpu.VMEM((width, width), jnp.float32), pltpu.VMEM((width, width), jnp.float32),
             pltpu.VMEM((NB, NB), jnp.float32), pltpu.VMEM((NB, NB), jnp.float32),
-            dma((2,)), dma((PANELS,)), dma((4,)), dma((2, CHUNKS)), dma((4,)), dma((pieces,)),
+            dma((2,)), dma((PANELS,)), dma((4,)), dma((2, CHUNKS)), dma((4,)), dma((pieces,)), dma(()),
         ],
-        compiler_params=pltpu.CompilerParams(collective_id=0, has_side_effects=True, vmem_limit_bytes=30 << 20),
+        compiler_params=pltpu.CompilerParams(collective_id=0, has_side_effects=True, vmem_limit_bytes=50 << 20),
     )(mine)
 
 
 def per_device(mine):
-    panel, other, rest, l, logdet = panel_step(mine)
-    width = mine.shape[0]
-    across = pl.BlockSpec((width, width), lambda s: (0, s))
-    whole = pl.BlockSpec((width, width), lambda s: (0, 0))
-    block = pl.pallas_call(
-        update_kernel,
-        grid=(mine.shape[1] // width,),
-        out_shape=jax.ShapeDtypeStruct(mine.shape, jnp.float32),
-        in_specs=[across, whole, across, whole],
-        out_specs=across,
-        compiler_params=pltpu.CompilerParams(vmem_limit_bytes=16 << 20),
-    )(rest, panel, other, l)
+    block, logdet = panel_step(mine)
     return block, logdet[0, 0]
 
 

time: 45.9 us -> 44 us (0.959)
  Pallas kernels: 42.3 us -> 40.7 us
    pallas_call x2 -> x1, Pallas kernels: 42.3 us -> 40.7 us  [panel_step(): pl.pallas_call(panel_kernel, out_shape=(jax.ShapeDtypeStruct(wide, jnp.fl...]
    unnamed x2 -> x1, local copies, waits for them, and re-layouts: 1.58 us -> 1.32 us
where the time goes in v7:
time: 44 us; the launch traced here: 43.8 us
  Pallas kernels  40.7 us (93%)
  between operations  1.8 us (4%)
  local copies, waits for them, and re-layouts  1.32 us (3%)
    pallas_call x1, Pallas kernels, panel_step(): pl.pallas_call(panel_kernel, out_shape=(jax.ShapeDtypeStruct(wide, jnp.fl...  40.7 us
    unnamed x1, local copies, waits for them, and re-layouts  1.32 us

profile of v7, /device:TPU:25, one launch (start us, length us, event | category | flops | bytes accessed | tf_op | source)
XLA Modules:
  0.0 43.8 jit_solution(12867632925700625185)
XLA Ops:
  0.6 40.7 %shard_map.30 = (f32[512,1024]{1,0:T(8,128)S(1)}, f32[1,128]{1,0:T(1,128)S(1)}) custom-call(f32[512,1024]{1,0:T(8,128)} %mine_ref.1), custom_call_target="tpu_custom_call" | custom-call | tf_op jit(solution)/shard_map/pallas_call | solution.py:482
  41.3 1.3 %copy.5 = f32[512,1024]{1,0:T(8,128)} copy(f32[512,1024]{1,0:T(8,128)S(1)} %get-tuple-element.8) | data formatting | bytes 4194304

commit v8 on v7

--- a/solution.py
+++ b/solution.py
@@ -265,11 +265,11 @@
     def cols_wait(n, i):
         cols_first(n, i).wait_recv()
 
-    def arrived(e):
+    def arrived(first, last):
         for n in range(2):
             @pl.when(jnp.logical_not(relays[n]) & ((c > 0) | (n == 1)))
             def _():
-                for i in range((e - half) // piece, e // piece):
+                for i in range(first // piece, last // piece):
                     cols_wait(n, i)
 
     half = width // 2
@@ -296,6 +296,15 @@
     def finish(at):
         block_row(width, at)
         rest_ref[:, at] = rest_ref[:, at] - dot_nn(panel_ref[:, half:], other_ref[half:, at])
+
+    def finish_late(at):
+        last = width - NB
+        arrived(half, last)
+        other_ref[half:, at] = dot_nn(w_ref[half:, :last], cols_ref[:last, at])
+        rest_ref[:, at] = rest_ref[:, at] - dot_nn(panel_ref[:, half:last], other_ref[half:last, at])
+        arrived(last, width)
+        other_ref[last:, at] = other_ref[last:, at] + dot_nn(w_ref[last:, last:], cols_ref[last:, at])
+        rest_ref[:, at] = rest_ref[:, at] - dot_nn(panel_ref[:, last:], other_ref[last:, at])
 
     for p in range(steps):
         if p * NB % half == 0 and half > NB:
@@ -406,7 +415,7 @@
                 def _():
                     w_arrive(0, first_half)
                     panel_arrive()
-                    arrived(half)
+                    arrived(0, half)
 
             if MIDDLE <= i < MIDDLE + len(items):
                 pl.when(between)(items[i - MIDDLE])
@@ -420,7 +429,7 @@
         def _():
             w_arrive(0, first_half)
             panel_arrive()
-            arrived(half)
+            arrived(0, half)
             block_row(half)
             panel(half)
             update()
@@ -436,8 +445,11 @@
             @pl.when(x == n)
             def _():
                 finish(slice(n * width, (n + 1) * width))
-                arrived(width)
-                finish(slice((1 - n) * width, (2 - n) * width))
+                if n == 0:
+                    finish_late(slice(width, 2 * width))
+                else:
+                    arrived(half, width)
+                    finish(slice(0, width))
 
         @pl.when(c == 0)
         def _():

time: 44 us -> 43.6 us (level)
  no operation moved by 1% of the time
where the time goes in v8:
time: 43.6 us; the launch traced here: 43.5 us
  Pallas kernels  40.4 us (93%)
  between operations  1.8 us (4%)
  local copies, waits for them, and re-layouts  1.32 us (3%)
    pallas_call x1, Pallas kernels, panel_step(): pl.pallas_call(panel_kernel, out_shape=(jax.ShapeDtypeStruct(wide, jnp.fl...  40.4 us
    unnamed x1, local copies, waits for them, and re-layouts  1.32 us

profile of v8, /device:TPU:25, one launch (start us, length us, event | category | flops | bytes accessed | tf_op | source)
XLA Modules:
  0.0 43.5 jit_solution(11141231586164841791)
XLA Ops:
  0.6 40.4 %shard_map.30 = (f32[512,1024]{1,0:T(8,128)S(1)}, f32[1,128]{1,0:T(1,128)S(1)}) custom-call(f32[512,1024]{1,0:T(8,128)} %mine_ref.1), custom_call_target="tpu_custom_call" | custom-call | tf_op jit(solution)/shard_map/pallas_call | solution.py:494
  41.0 1.3 %copy.5 = f32[512,1024]{1,0:T(8,128)} copy(f32[512,1024]{1,0:T(8,128)S(1)} %get-tuple-element.8) | data formatting | bytes 4194304

commit v9 on v8

--- a/solution.py
+++ b/solution.py
@@ -420,10 +420,11 @@
             if MIDDLE <= i < MIDDLE + len(items):
                 pl.when(between)(items[i - MIDDLE])
 
-        @pl.when(patient & odd)
-        def _():
-            for m in range(len(pieces)):
-                w_relay(m)
+        for first, last, plane in ((0, FOLLOW, odd), (FOLLOW, len(pieces), c == 1)):
+            @pl.when(patient & plane)
+            def _():
+                for m in range(first, last):
+                    w_relay(m)
 
         @pl.when(jnp.logical_not(between))
         def _():
@@ -434,7 +435,7 @@
             panel(half)
             update()
 
-        @pl.when(odd & (c > 1) & jnp.logical_not(patient))
+        @pl.when(odd & (c > 1))
         def _():
             for m in range(FOLLOW, len(pieces)):
                 w_relay(m)

time: 43.6 us -> 43.6 us (level)
  no operation moved by 1% of the time
where the time goes in v9:
time: 43.6 us; the launch traced here: 43.5 us
  Pallas kernels  40.4 us (93%)
  between operations  1.8 us (4%)
  local copies, waits for them, and re-layouts  1.32 us (3%)
    pallas_call x1, Pallas kernels, panel_step(): pl.pallas_call(panel_kernel, out_shape=(jax.ShapeDtypeStruct(wide, jnp.fl...  40.4 us
    unnamed x1, local copies, waits for them, and re-layouts  1.32 us

profile of v9, /device:TPU:25, one launch (start us, length us, event | category | flops | bytes accessed | tf_op | source)
XLA Modules:
  0.0 43.5 jit_solution(16226241382376891935)
XLA Ops:
  0.6 40.4 %shard_map.30 = (f32[512,1024]{1,0:T(8,128)S(1)}, f32[1,128]{1,0:T(1,128)S(1)}) custom-call(f32[512,1024]{1,0:T(8,128)} %mine_ref.1), custom_call_target="tpu_custom_call" | custom-call | tf_op jit(solution)/shard_map/pallas_call | solution.py:495
  41.0 1.3 %copy.5 = f32[512,1024]{1,0:T(8,128)} copy(f32[512,1024]{1,0:T(8,128)S(1)} %get-tuple-element.8) | data formatting | bytes 4194304
